TPU v7x, 32 devices: a whole 2x2x4 slice. The times are simulated.
32 devices in a mesh: dp: 4 (over z), section: 2 (over core), space: 4 (over y, x).
Axes of the slice: x: 2, y: 2, z: 4, core: 2. Of those that a mesh axis runs over, the one named last changes fastest.
Arguments:
- latents: bfloat16 [16, 96, 192, 320], P('dp', 'space'), parts along dimension 0, may hold values from -16 to 16
- kernels: bfloat16 [2, 3, 3, 320, 320], P('section'), may hold values from -0.109375 to 0.109375
- norm_gain: float32 [2, 320], P('section'), may hold values from 0.25 to 1.75
- norm_bias: float32 [2, 320], P('section'), may hold values from -3 to 3
- conv_bias: float32 [2, 320], P('section'), may hold values from -3 to 3
Outputs:
- skips: bfloat16 [2, 16, 96, 192, 320], P('section', 'dp', 'space'), parts along dimension 1
There are 4 independent parts, one for each index of `dp`. A program takes and returns all parts, laid end to end along the dimension named above; an argument that names none is the same for every part. Nothing has to cross between parts.
All inputs are finite; a program needn't handle non-finite values.
Results may differ from a plain program's by a relative error of at most 0.01.
Values may be sent and summed in bfloat16 or wider, within the bound.
A program may use at most 128 MiB of HBM per device.

v0:
```python
import jax
import jax.numpy as jnp
from jax import lax
from jax.sharding import PartitionSpec as P

GROUPS = 32


def padded_2(array, sides, width):
    for axis, dim in sides:
        size, length = (lax.axis_size(axis), array.shape[dim])
        up = [(i, (i + 1) % size) for i in range(size - 1)]
        down = [(j, i) for i, j in up]
        last = lax.slice_in_dim(array, length - width, length, axis=dim)
        initial = lax.slice_in_dim(array, 0, width, axis=dim)
        before = lax.ppermute(last, axis, up)
        after = lax.ppermute(initial, axis, down)
        array = jnp.concatenate([before, array, after], axis=dim)
    return array


def group_moments(inputs):
    batch_count, local_rows, columns, channels = inputs.shape
    members = local_rows * lax.axis_size("space") * columns * (channels // GROUPS)
    values = inputs.astype(jnp.float32).reshape(
        batch_count, local_rows * columns, GROUPS, channels // GROUPS
    )
    totals = lax.psum(jnp.sum(values, axis=(1, 3)), "space")
    group_mean = totals / members
    deviation = values - group_mean[:, None, :, None]
    spread = lax.psum(jnp.sum(deviation * deviation, axis=(1, 3)), "space")
    group_var = spread / members
    return (group_mean, lax.rsqrt(group_var + 1e-05))


def apply_layer(inputs, kernel, norm_gain, norm_shift, shift_bias, residual):
    batch_count, local_rows, columns, channels = inputs.shape
    group_mean, inv_spread = group_moments(inputs)
    padded = padded_2(inputs, (("space", 1),), 1)
    values = padded.astype(jnp.float32).reshape(
        batch_count, local_rows + 2, columns, GROUPS, channels // GROUPS
    )
    scaled = (values - group_mean[:, None, None, :, None]) * inv_spread[:, None, None, :, None]
    scaled = scaled.reshape(batch_count, local_rows + 2, columns, channels) * norm_gain + norm_shift
    activated = jax.nn.silu(scaled)
    space_index = lax.axis_index("space")
    row_place = lax.broadcasted_iota(jnp.int32, (1, local_rows + 2, 1, 1), 1)
    outside = jnp.logical_or(
        jnp.logical_and(space_index == 0, row_place == 0),
        jnp.logical_and(space_index == lax.axis_size("space") - 1, row_place == local_rows + 1),
    )
    normed = jnp.where(outside, 0.0, activated).astype(jnp.bfloat16)
    convolved = lax.conv_general_dilated(
        normed,
        kernel,
        (1, 1),
        ((0, 0), (1, 1)),
        dimension_numbers=("NHWC", "HWIO", "NHWC"),
        preferred_element_type=jnp.float32,
    )
    return (residual + convolved + shift_bias).astype(jnp.bfloat16)


def on_device(latents, kernels, norm_gain, norm_bias, conv_bias):
    section_count = lax.axis_size("section")
    section_index = lax.axis_index("section")
    sample_count = latents.shape[0]
    per_section = sample_count // section_count
    own = lax.dynamic_slice_in_dim(latents, section_index * per_section, per_section, 0)
    all_kernels, all_gains, all_shifts, all_biases = (
        lax.all_gather(kernels, "section", axis=0, tiled=True),
        lax.all_gather(norm_gain.astype(jnp.bfloat16), "section", axis=0, tiled=True).astype(
            norm_gain.dtype
        ),
        lax.all_gather(norm_bias.astype(jnp.bfloat16), "section", axis=0, tiled=True).astype(
            norm_bias.dtype
        ),
        lax.all_gather(conv_bias.astype(jnp.bfloat16), "section", axis=0, tiled=True).astype(
            conv_bias.dtype
        ),
    )
    first = apply_layer(
        own,
        all_kernels[0],
        all_gains[0],
        all_shifts[0],
        all_biases[0],
        jnp.zeros(own.shape, jnp.float32),
    )
    second = apply_layer(
        first, all_kernels[1], all_gains[1], all_shifts[1], all_biases[1], own.astype(jnp.float32)
    )
    stacked = jnp.stack([first, second])
    return lax.all_to_all(stacked, "section", split_axis=0, concat_axis=1, tiled=True)


def solution(mesh):
    return jax.shard_map(
        on_device,
        mesh=mesh,
        in_specs=(
            P("dp", "space", None, None),
            P("section", None, None, None, None),
            P("section", None),
            P("section", None),
            P("section", None),
        ),
        out_specs=P("section", "dp", "space", None, None),
        check_vma=False,
    )
```

profile of v0, /device:TPU:0, one launch (start us, length us, event | category | flops | bytes accessed | tf_op | source)
XLA Modules:
  0.0 418.2 jit_solution(17742653604822381069)
XLA Ops:
  27.6 6.8 %convert_reduce_fusion = f32[2,320]{1,0:T(2,128)S(1)} fusion(bf16[2,24,192,320]{3,2,1,0:T(8,128)(2,1)} %copy-done), kind=kLoop, calls=%fused_computation.2 | loop fusion | flops 5897600 | bytes 5900800 | tf_op jit(solution)/shard_map/reduce_sum | solution.py:28
  34.6 11.2 %psum.28 = f32[2,32]{1,0:T(2,128)S(1)} all-reduce(f32[2,32]{1,0:T(2,128)S(1)} %reduce_sum.51), channel_id=1, replica_groups=mesh['dp'=4,'section'=2,'space'=4] {'space'}, use_global_device_ids=true, to_apply=%region_2.0 | all-reduce | flops 64 | bytes 512 | tf_op jit(solution)/shard_map/psum | solution.py:28
  46.0 6.9 %fusion.4 = f32[2,320]{1,0:T(2,128)S(1)} fusion(f32[2,320]{1,0:T(2,128)S(1)} %sub.45, bf16[2,24,192,320]{3,2,1,0:T(8,128)(2,1)} %copy-done), kind=kLoop, calls=%fused_computation.12 | loop fusion | flops 11795840 | bytes 5903360 | tf_op jit(solution)/shard_map/reduce_sum | solution.py:31
  53.1 8.8 %psum.29 = f32[2,32]{1,0:T(2,128)S(1)} all-reduce(f32[2,32]{1,0:T(2,128)S(1)} %reduce_sum.54), channel_id=1, replica_groups=mesh['dp'=4,'section'=2,'space'=4] {'space'}, use_global_device_ids=true, to_apply=%region_5.6 | all-reduce | flops 64 | bytes 512 | tf_op jit(solution)/shard_map/psum | solution.py:31
  69.3 12.7 %fusion.7 = bf16[26,2,192,320]{3,0,2,1:T(8,128)(2,1)S(1)} fusion(bf16[2,1,192,320]{3,1,2,0:T(2,128)(2,1)S(1)} %copy.42, bf16[2,24,192,320]{3,1,2,0:T(8,128)(2,1)} %copy-done.2, bf16[2,1,192,320]{3,1,2,0:T(2,128)(2,1)S(1)} %copy.41, f32[320]{0:T(512)S(1)} %get-tuple-element.10, f32[320]{0:T(512)S(1)} %get-tuple-element.8, f32[2,320]{1,0:T(2,128)S(1)} %mul.67, ...), kind=kLoop, calls=%fused_computation.20 | loop fusion | flops 51118080 | bytes 12787226 | tf_op jit(solution)/shard_map/convert_element_type | solution.py:52
  82.1 35.5 %copy.60 = bf16[26,2,192,320]{3,1,2,0:T(2,128)(2,1)S(1)} copy(bf16[26,2,192,320]{3,0,2,1:T(8,128)(2,1)S(1)} %fusion.7) | data formatting | bytes 12779520
  117.6 9.1 %pad.clone = bf16[26,2,200,320]{3,1,2,0:T(2,128)(2,1)S(1)} pad(bf16[26,2,192,320]{3,1,2,0:T(2,128)(2,1)S(1)} %copy.60, bf16[]{:T(256)} %constant.38), padding=0_0x0_0x1_7x0_0 | pad | bytes 13045762 | tf_op jit(solution)/shard_map/convert_element_type | solution.py:52
  127.1 9.6 %fusion.9 = bf16[26,2,8,27,320]{4,1,3,2,0:T(2,128)(2,1)} fusion(bf16[26,2,7,2,320]{4,1,3,2,0:T(2,128)(2,1)S(1)} %slice.68, bf16[26,2,8,25,320]{4,1,3,2,0:T(2,128)(2,1)S(1)} %bitcast.61), kind=kLoop, calls=%fused_computation.22 | loop fusion | flops 21565440 | bytes 14310400 | tf_op jit(solution)/shard_map/conv_general_dilated | solution.py:53
  136.7 33.9 %add_convert_fusion = bf16[24,16,25,320]{3,1,2,0:T(8,128)(2,1)S(1)} fusion(bf16[26,2,8,27,320]{4,1,3,2,0:T(2,128)(2,1)} %fusion.9, f32[320]{0:T(512)S(1)} %get-tuple-element.6, pred[16,25]{0,1:T(8,128)(4,1)S(1)} %copy-done.8, bf16[2,3,3,320,320]{4,3,2,1,0:T(8,128)(2,1)} %all-gather.5.cloned.1.call-done), kind=kOutput, calls=%fused_computation.10 | convolution fusion | flops 17703936000 | bytes 16983696 | tf_op jit(solution)/shard_map/conv_general_dilated | solution.py:53
  170.6 7.1 %copy.52 = f32[24,16,25,320]{3,0,2,1:T(8,128)} copy(bf16[24,16,25,320]{3,1,2,0:T(8,128)(2,1)S(1)} %add_convert_fusion) | data formatting | bytes 18432000 | tf_op jit(solution)/shard_map/convert_element_type | solution.py:25
  189.3 8.2 %psum.30 = f32[2,32]{1,0:T(2,128)S(1)} all-reduce(f32[2,32]{1,0:T(2,128)S(1)} %reduce_sum.72), channel_id=1, replica_groups=mesh['dp'=4,'section'=2,'space'=4] {'space'}, use_global_device_ids=true, to_apply=%region_8.9 | all-reduce | flops 64 | bytes 512 | tf_op jit(solution)/shard_map/psum | solution.py:28
  199.9 7.3 %fusion.2 = f32[24,16,25,320]{3,1,2,0:T(8,128)} fusion(f32[24,16,25,320]{3,0,2,1:T(8,128)S(1)} %bitcast.53, bf16[24,16,25,320]{3,1,2,0:T(8,128)(2,1)S(1)} %bitcast.52), kind=kLoop, calls=%fused_computation.9 | loop fusion | flops 9216000 | bytes 30720000 | tf_op jit(solution)/shard_map/mul | solution.py:31
  207.2 15.1 %copy.54 = f32[24,16,25,320]{3,0,2,1:T(8,128)} copy(f32[24,16,25,320]{3,1,2,0:T(8,128)} %fusion.2) | data formatting | bytes 24576000 | tf_op jit(solution)/shard_map/mul | solution.py:31
  222.3 9.2 %slice_bitcast_fusion.1 = (bf16[1,2,24,192,320]{4,2,3,1,0:T(8,128)(2,1)}, bf16[2,24,192,320]{3,1,2,0:T(8,128)(2,1)}) fusion(bf16[24,2,200,320]{3,0,2,1:T(8,128)(2,1)} %bitcast.62), kind=kLoop, calls=%fused_computation.29 | loop fusion | bytes 17694720 | tf_op jit(solution)/shard_map/stack | solution.py:93
  242.6 10.4 %psum.31 = f32[2,32]{1,0:T(2,128)S(1)} all-reduce(f32[2,32]{1,0:T(2,128)S(1)} %reduce_sum.75), channel_id=1, replica_groups=mesh['dp'=4,'section'=2,'space'=4] {'space'}, use_global_device_ids=true, to_apply=%region_11.12 | all-reduce | flops 64 | bytes 512 | tf_op jit(solution)/shard_map/psum | solution.py:31
  254.2 12.7 %fusion.8 = bf16[26,2,192,320]{3,0,2,1:T(8,128)(2,1)S(1)} fusion(bf16[2,1,192,320]{3,1,2,0:T(2,128)(2,1)S(1)} %copy.51, bf16[2,24,192,320]{3,1,2,0:T(8,128)(2,1)} %get-tuple-element.12, bf16[2,1,192,320]{3,1,2,0:T(2,128)(2,1)S(1)} %copy.50, f32[320]{0:T(512)S(1)} %get-tuple-element.9, f32[320]{0:T(512)S(1)} %get-tuple-element.7, f32[2,320]{1,0:T(2,128)S(1)} %mul.76, ...), kind=kLoop, calls=%fused_computation.21 | loop fusion | flops 51118080 | bytes 12787226 | tf_op jit(solution)/shard_map/convert_element_type | solution.py:52
  266.9 35.5 %copy.61 = bf16[26,2,192,320]{3,1,2,0:T(2,128)(2,1)S(1)} copy(bf16[26,2,192,320]{3,0,2,1:T(8,128)(2,1)S(1)} %fusion.8) | data formatting | bytes 12779520
  302.4 9.1 %pad.2.clone = bf16[26,2,200,320]{3,1,2,0:T(2,128)(2,1)S(1)} pad(bf16[26,2,192,320]{3,1,2,0:T(2,128)(2,1)S(1)} %copy.61, bf16[]{:T(256)} %constant.38), padding=0_0x0_0x1_7x0_0 | pad | bytes 13045762 | tf_op jit(solution)/shard_map/convert_element_type | solution.py:52
  312.0 8.8 %fusion.10 = bf16[26,2,8,27,320]{4,1,3,2,0:T(2,128)(2,1)S(1)} fusion(bf16[26,2,7,2,320]{4,1,3,2,0:T(2,128)(2,1)S(1)} %slice.80, bf16[26,2,8,25,320]{4,1,3,2,0:T(2,128)(2,1)S(1)} %bitcast.59), kind=kLoop, calls=%fused_computation.23 | loop fusion | flops 21565440 | bytes 14310400 | tf_op jit(solution)/shard_map/conv_general_dilated | solution.py:53
  320.8 33.1 %convolution_select_fusion = f32[24,16,25,320]{3,1,2,0:T(8,128)} fusion(bf16[26,2,8,27,320]{4,1,3,2,0:T(2,128)(2,1)S(1)} %fusion.10, pred[16,25]{0,1:T(8,128)(4,1)S(1)} %copy-done.8, bf16[2,3,3,320,320]{4,3,2,1,0:T(8,128)(2,1)S(1)} %bitcast.64), kind=kOutput, calls=%fused_computation.19 | convolution fusion | flops 17697792000 | bytes 23130112 | tf_op jit(solution)/shard_map/conv_general_dilated | solution.py:53
  353.9 15.1 %copy.57 = f32[24,16,25,320]{3,0,2,1:T(8,128)} copy(f32[24,16,25,320]{3,1,2,0:T(8,128)} %convolution_select_fusion) | data formatting | bytes 24576000 | tf_op jit(solution)/shard_map/conv_general_dilated | solution.py:53
  369.0 13.2 %fusion.15 = bf16[1,2,24,192,320]{4,2,3,1,0:T(8,128)(2,1)S(1)} fusion(f32[24,2,200,320]{3,0,2,1:T(8,128)} %bitcast.54, f32[320]{0:T(512)S(1)} %copy-done.4, bf16[2,24,192,320]{3,2,1,0:T(8,128)(2,1)} %copy-done), kind=kLoop, calls=%fused_computation.28 | loop fusion | flops 11796480 | bytes 23594240 | tf_op jit(solution)/shard_map/stack | solution.py:93
  389.0 15.1 %all_to_all.12 = bf16[2,2,24,192,320]{4,2,3,1,0:T(8,128)(2,1)S(1)} all-to-all(bf16[2,2,24,192,320]{4,2,3,1,0:T(8,128)(2,1)S(1)} %pad_maximum_fusion), channel_id=1, replica_groups=mesh['dp'=4,'section'=2,'space'=4] {'section'}, dimensions={0} | all-to-all | bytes 23592960 | tf_op jit(solution)/shard_map/all_to_all | solution.py:94
  404.1 6.9 %copy.58 = bf16[1,4,24,192,320]{4,3,2,1,0:T(8,128)(2,1)} copy(bf16[1,4,24,192,320]{4,2,3,1,0:T(8,128)(2,1)S(1)} %bitcast.57) | data formatting | bytes 23592960 | tf_op jit(solution)/shard_map/all_to_all | solution.py:94
  (95 shorter events, 62.4 us)
Async XLA Ops:
  6.5 130.2 %all-gather.5.cloned.1.call-start = ((), (), s32[]{:S(2)}) async-start(), calls=%async_computation.1 | async-start | bytes 6635520 | tf_op jit(solution)/shard_map/all_gather | solution.py:71
  10.3 2.9 copy-start
  13.2 48.8 %copy-start.5 = (f32[1,320]{1,0:T(1,128)S(1)}, f32[1,320]{1,0:T(1,128)}, u32[]{:S(2)}) copy-start(f32[1,320]{1,0:T(1,128)} %param.8) | copy-start | bytes 3844
  13.2 50.7 %copy-start.6 = (f32[1,320]{1,0:T(1,128)S(1)}, f32[1,320]{1,0:T(1,128)}, u32[]{:S(2)}) copy-start(f32[1,320]{1,0:T(1,128)} %param.7) | copy-start | bytes 3844
  13.2 50.7 %copy-start.7 = (f32[1,320]{1,0:T(1,128)S(1)}, f32[1,320]{1,0:T(1,128)}, u32[]{:S(2)}) copy-start(f32[1,320]{1,0:T(1,128)} %param.9) | copy-start | bytes 3844
  17.4 3.0 copy-start.2
  21.3 47.1 %collective-permute-start = (bf16[2,1,192,320]{3,2,1,0:T(8,128)(2,1)S(1)}, bf16[2,1,192,320]{3,2,1,0:T(8,128)(2,1)S(1)}, u32[]{:S(2)}, u32[]{:S(2)}) collective-permute-start(bf16[2,1,192,320]{3,2,1,0:T(8,128)(2,1)S(1)} %copy.39), channel_id=1, source_target_pairs={{0,1},{1,2},{2,3},{4,5},{5,6},{6,7},{8,9},{9,10},{10,11},{12,13},{... | collective-permute-start | bytes 737288 | tf_op jit(solution)/shard_map/ppermute | solution.py:16
  26.3 42.6 %collective-permute-start.1 = (bf16[2,1,192,320]{3,2,1,0:T(8,128)(2,1)S(1)}, bf16[2,1,192,320]{3,2,1,0:T(8,128)(2,1)S(1)}, u32[]{:S(2)}, u32[]{:S(2)}) collective-permute-start(bf16[2,1,192,320]{3,2,1,0:T(8,128)(2,1)S(1)} %copy.40), channel_id=1, source_target_pairs={{1,0},{2,1},{3,2},{5,4},{6,5},{7,6},{9,8},{10,9},{11,10},{13,12},{... | collective-permute-start | bytes 737288 | tf_op jit(solution)/shard_map/ppermute | solution.py:17
  117.6 19.2 %copy-start.8 = (pred[16,25]{0,1:T(8,128)(4,1)S(1)}, pred[16,25]{0,1:T(8,128)(4,1)}, u32[]{:S(2)}) copy-start(pred[16,25]{0,1:T(8,128)(4,1)} %constant.46) | copy-start | bytes 1204
  170.6 11.8 %copy-start.1 = (bf16[24,16,25,320]{3,1,2,0:T(8,128)(2,1)}, bf16[24,16,25,320]{3,1,2,0:T(8,128)(2,1)S(1)}, u32[]{:S(2)}) copy-start(bf16[24,16,25,320]{3,1,2,0:T(8,128)(2,1)S(1)} %add_convert_fusion) | copy-start | bytes 18432004
  183.2 15.5 %slice-start = ((s8[7372800]{0:T(1024)(128)(4,1)}), s8[3178496]{0:T(1024)(128)(4,1)S(1)}, s32[]{:S(2)}) async-start(s8[7372800]{0:T(1024)(128)(4,1)} %bitcast.51), calls=%async_computation.2 | async-start | bytes 6356992
  197.7 2.2 slice-start.1
  222.3 9.2 %copy-start.3 = (bf16[1,16,25,320]{3,1,2,0:T(8,128)(2,1)S(1)}, bf16[1,16,25,320]{3,1,2,0:T(8,128)(2,1)}, u32[]{:S(2)}) copy-start(bf16[1,16,25,320]{3,1,2,0:T(8,128)(2,1)} %get-tuple-element.13) | copy-start | bytes 768004
  231.8 21.4 %collective-permute-start.2 = (bf16[2,1,192,320]{3,2,1,0:T(8,128)(2,1)S(1)}, bf16[2,1,192,320]{3,2,1,0:T(8,128)(2,1)S(1)}, u32[]{:S(2)}, u32[]{:S(2)}) collective-permute-start(bf16[2,1,192,320]{3,2,1,0:T(8,128)(2,1)S(1)} %slice_bitcast_fusion.8), channel_id=1, source_target_pairs={{0,1},{1,2},{2,3},{4,5},{5,6},{6,7},{8,9},{9,10},{10,11},{12,13},{... | collective-permute-start | bytes 737288 | tf_op jit(solution)/shard_map/ppermute | solution.py:16
  235.4 18.3 %collective-permute-start.3 = (bf16[2,1,192,320]{3,2,1,0:T(8,128)(2,1)S(1)}, bf16[2,1,192,320]{3,2,1,0:T(8,128)(2,1)S(1)}, u32[]{:S(2)}, u32[]{:S(2)}) collective-permute-start(bf16[2,1,192,320]{3,2,1,0:T(8,128)(2,1)S(1)} %slice_bitcast_fusion.7), channel_id=1, source_target_pairs={{1,0},{2,1},{3,2},{5,4},{6,5},{7,6},{9,8},{10,9},{11,10},{13,12},{... | collective-permute-start | bytes 737288 | tf_op jit(solution)/shard_map/ppermute | solution.py:17
  302.4 18.3 %slice-start.2 = ((s8[4423680]{0:T(1024)(128)(4,1)}), s8[4194304]{0:T(1024)(128)(4,1)S(1)}, s32[]{:S(2)}) async-start(s8[4423680]{0:T(1024)(128)(4,1)} %bitcast.63), calls=%async_computation.4 | async-start | bytes 8388608
  311.9 8.8 %slice-start.3 = ((s8[4423680]{0:T(1024)(128)(4,1)}), s8[229376]{0:T(1024)(128)(4,1)S(1)}, s32[]{:S(2)}) async-start(s8[4423680]{0:T(1024)(128)(4,1)} %bitcast.63), calls=%async_computation.5 | async-start | bytes 458752
  353.8 15.2 %copy-start.4 = (f32[320]{0:T(512)S(1)}, f32[320]{0:T(512)}, u32[]{:S(2)}) copy-start(f32[320]{0:T(512)} %get-tuple-element.5) | copy-start | bytes 3844
Sparse Core Ops, SparseCore 0:
  27.7 16.3 all-gather.4
where the time goes:
time: 427 us; the launch traced here: 418 us
  local copies, waits for them, and re-layouts  170 us (40%)
  other arithmetic  96.9 us (23%)
  matrix products  67 us (16%)
  blocking collectives  59.3 us (14%)
  between operations  14.3 us (3%)
  starting transfers between devices  10.7 us (3%)
    unnamed x29, local copies, waits for them, and re-layouts  82.2 us
    conv_general_dilated x2, matrix products, apply_layer(): lax.conv_general_dilated(normed, kernel, (1, 1), ((0, 0), (1, 1)), dimens...  67 us
    convert_element_type x2, other arithmetic, apply_layer(): normed = jnp.where(outside, 0.0, activated).astype(jnp.bfloat16)  25.5 us
    another operation x2, other arithmetic, on_device(): stacked = jnp.stack([first, second])  19.9 us
    psum x2, blocking collectives, group_moments(): totals = lax.psum(jnp.sum(values, axis=(1, 3)), 'space')  19.5 us
    psum x2, blocking collectives, group_moments(): spread = lax.psum(jnp.sum(deviation * deviation, axis=(1, 3)), 'space')  19.2 us
    conv_general_dilated x2, other arithmetic, apply_layer(): lax.conv_general_dilated(normed, kernel, (1, 1), ((0, 0), (1, 1)), dimens...  18.4 us
    convert_element_type x2, local copies, waits for them, and re-layouts, apply_layer(): normed = jnp.where(outside, 0.0, activated).astype(jnp.bfloat16)  18.3 us
  transfers between devices with their start and end apart: 5, of which 0 were waited for; matrix products, arithmetic and copies ran while one was open for 22% of the time, Pallas kernels for 0%

commit v1 on v0

v1 whole, which is shorter than its diff:
```python
import functools

import jax
import jax.numpy as jnp
from jax import lax
from jax.experimental import pallas as pl
from jax.experimental.pallas import tpu as pltpu
from jax.sharding import PartitionSpec as P

GROUPS = 32
EPS = 1e-05
MAIN = 256
VMEM_LIMIT = 60 * 1024 * 1024


def pick_block(rows):
    return max(d for d in range(1, 9) if rows % d == 0)


def column_pieces(channels):
    main = channels // MAIN * MAIN
    tail = channels - main
    return main, tail, 3 * main


def packed_width(channels):
    return -(-3 * channels // MAIN) * MAIN


def pack_kernel(k_ref, w_ref, buf):
    channels = k_ref.shape[-1]
    main, tail, base = column_pieces(channels)
    buf[...] = jnp.zeros_like(buf)
    for dr in range(3):
        for dc in range(3):
            tap = k_ref[dr, dc]
            for klo, khi, kdst in ((0, main, dc * main), (main, channels, base + dc * tail)):
                for nlo, nhi, ndst in ((0, main, dr * main), (main, channels, base + dr * tail)):
                    buf[kdst:kdst + khi - klo, ndst:ndst + nhi - nlo] = tap[klo:khi, nlo:nhi]
    w_ref[...] = buf[...]


def pack_weights(kernel):
    channels = kernel.shape[-1]
    width = packed_width(channels)
    return pl.pallas_call(
        pack_kernel,
        out_shape=jax.ShapeDtypeStruct((width, width), jnp.bfloat16),
        scratch_shapes=[pltpu.VMEM((width, width), jnp.bfloat16)],
        compiler_params=pltpu.CompilerParams(vmem_limit_bytes=VMEM_LIMIT),
        cost_estimate=pl.CostEstimate(flops=0, bytes_accessed=6 * width * width, transcendentals=0),
        name="pack",
    )(kernel)


def row_moments(values):
    mean = jnp.sum(values, axis=0, keepdims=True) * (1.0 / values.shape[0])
    deviation = values - mean
    return mean, jnp.sum(deviation * deviation, axis=0, keepdims=True)


def moments_kernel(scal, x_ref, m_ref):
    for i in range(x_ref.shape[1]):
        mean, spread = row_moments(x_ref[0, i].astype(jnp.float32))
        m_ref[0, 0, 0, i:i + 1, :] = mean
        m_ref[0, 1, 0, i:i + 1, :] = spread


def moments(scal, latents, count):
    _, rows, columns, channels = latents.shape
    block = pick_block(rows)
    return pl.pallas_call(
        moments_kernel,
        grid_spec=pltpu.PrefetchScalarGridSpec(
            num_scalar_prefetch=1,
            grid=(count, rows // block),
            in_specs=[
                pl.BlockSpec((1, block, columns, channels), lambda s, c, scal: (scal[3] + s, c, 0, 0))
            ],
            out_specs=pl.BlockSpec((1, 2, 1, block, channels), lambda s, c, scal: (s, 0, c, 0, 0)),
        ),
        out_shape=jax.ShapeDtypeStruct((count, 2, rows // block, block, channels), jnp.float32),
        compiler_params=pltpu.CompilerParams(vmem_limit_bytes=VMEM_LIMIT),
        cost_estimate=pl.CostEstimate(
            flops=0, bytes_accessed=count * rows * columns * channels * 2, transcendentals=0
        ),
        name="moments",
    )(scal, latents)


def conv_kernel(stage, parts, *refs):
    scal, x_ref, top_ref, bot_ref = refs[:4]
    stat_refs = refs[4:4 + parts]
    par_ref, wa_ref, wb_ref = refs[4 + parts:7 + parts]
    rest = refs[7 + parts:]
    if stage == 0:
        y_ref, m_ref = rest[:2]
        rest = rest[2:]
    else:
        if len(rest) > 13:
            rest_in, rest = rest[:3], rest[3:]
        else:
            rest_in, rest = rest[:2], rest[2:]
        res_ref, own_ref = rest_in[:2]
        keep_ref, y_ref = rest[:2]
        rest = rest[2:]
    w_ref, act_ref, lhs_a, lhs_b, p_ref, carry_ref, next_ref, ab_ref, sem = rest
    step, last = pl.program_id(0), pl.num_programs(0) - 1
    block, columns, channels = x_ref.shape[1:]
    main, tail, base = column_pieces(channels)
    width = w_ref.shape[0]
    unit = -(-block // 2)

    @pl.when(step == 0)
    def _():
        own_first = scal[0] == stage
        copy_a = pltpu.make_async_copy(wa_ref, w_ref, sem.at[0])
        copy_b = pltpu.make_async_copy(wb_ref, w_ref, sem.at[0])

        @pl.when(own_first)
        def _():
            copy_a.start()

        @pl.when(jnp.logical_not(own_first))
        def _():
            copy_b.start()

        act_ref[:, 0:8, :] = jnp.zeros((act_ref.shape[0], 8, channels), jnp.float32)
        act_ref[:, columns + 8:columns + 16, :] = jnp.zeros((act_ref.shape[0], 8, channels), jnp.float32)
        per_group = channels // GROUPS
        row_id = lax.broadcasted_iota(jnp.int32, (channels, channels), 0).astype(jnp.float32)
        col_id = lax.broadcasted_iota(jnp.int32, (channels, channels), 1).astype(jnp.float32)
        same = jnp.floor((row_id + 0.5) * (1.0 / per_group)) == jnp.floor((col_id + 0.5) * (1.0 / per_group))
        members = jnp.where(same, 1.0, 0.0).astype(jnp.float32)

        def over_groups(value):
            return jnp.dot(
                jnp.broadcast_to(value, (8, channels)), members,
                precision=lax.Precision.HIGHEST, preferred_element_type=jnp.float32,
            )[0:1]

        chunks, rows_of = stat_refs[0].shape[-3:-1]
        cells = parts * chunks * rows_of
        total = jnp.zeros((1, channels), jnp.float32)
        for ref in stat_refs:
            for j in range(chunks):
                total += jnp.sum(ref[0, 0, j], axis=0, keepdims=True)
        mean = over_groups(total) * (1.0 / (cells * per_group))
        spread = jnp.zeros((1, channels), jnp.float32)
        for ref in stat_refs:
            for j in range(chunks):
                away = ref[0, 0, j] - mean
                spread += jnp.sum(away * away * float(columns) + ref[0, 1, j], axis=0, keepdims=True)
        var = over_groups(spread) * (1.0 / (cells * per_group * columns))
        inv = lax.rsqrt(var + EPS)
        ab_ref[0:1, :] = mean
        ab_ref[1:2, :] = 0.5 * inv * par_ref[0:1, :]
        ab_ref[2:3, :] = 0.5 * par_ref[1:2, :]
        copy_a.wait()

    def activate(values, slot, lhs, place, valid=None):
        half = (values.astype(jnp.float32) - ab_ref[0:1, :]) * ab_ref[1:2, :] + ab_ref[2:3, :]
        act = half + half * jnp.tanh(half)
        if valid is not None:
            act = jnp.where(valid, act, 0.0)
        act_ref[slot, 8:columns + 8, :] = act
        rows = slice(place * columns, (place + 1) * columns)
        for dc in range(3):
            lhs[rows, dc * main:(dc + 1) * main] = act_ref[slot, 7 + dc:7 + dc + columns, 0:main].astype(jnp.bfloat16)
        tails = [act_ref[slot, 7 + dc:7 + dc + columns, main:channels] for dc in range(3)]
        tails.append(jnp.zeros((columns, width - base - 3 * tail), jnp.float32))
        lhs[rows, base:width] = jnp.concatenate(tails, axis=1).astype(jnp.bfloat16)

    def edge(ref, valid, tap, dst):
        activate(ref[...], 0, lhs_a, 0, valid)
        left = lhs_a[0:columns, :]
        dst[:, 0:main] = jnp.dot(left, w_ref[:, tap * main:(tap + 1) * main], preferred_element_type=jnp.float32)
        ends = jnp.dot(left, w_ref[:, base:width], preferred_element_type=jnp.float32)
        dst[:, main:channels] = ends[:, tap * tail:(tap + 1) * tail]

    @pl.when(step == 0)
    def _():
        edge(top_ref, scal[1] == 1, 0, carry_ref)

    @pl.when(step == last)
    def _():
        edge(bot_ref, scal[2] == 1, 2, next_ref)

    now = step % 2
    before = 1 - now

    @pl.when(step < last)
    def _():
        for u, lhs in ((0, lhs_a), (1, lhs_b)):
            lo, hi = u * unit, min((u + 1) * unit, block)
            if hi <= lo:
                continue
            for i in range(lo, hi):
                activate(x_ref[0, i], i, lhs, i - lo)
            p_ref[now, lo * columns:hi * columns, :] = jnp.dot(
                lhs[0:(hi - lo) * columns, :], w_ref[...], preferred_element_type=jnp.float32
            )
        next_ref[:, 0:main] = p_ref[now, 0:columns, 2 * main:3 * main]
        next_ref[:, main:channels] = p_ref[now, 0:columns, base + 2 * tail:base + 3 * tail]

    @pl.when(step > 0)
    def _():
        shift = par_ref[2:3, :]

        def tap_of(i, tap):
            rows = slice(i * columns, (i + 1) * columns)
            return (
                p_ref[before, rows, tap * main:(tap + 1) * main],
                p_ref[before, rows, base + tap * tail:base + (tap + 1) * tail],
            )

        def whole(ref):
            return ref[:, 0:main], ref[:, main:channels]

        for i in range(block):
            above = whole(carry_ref) if i == 0 else tap_of(i - 1, 0)
            middle = tap_of(i, 1)
            below = whole(next_ref) if i == block - 1 else tap_of(i + 1, 2)
            for j, (lo, hi) in enumerate(((0, main), (main, channels))):
                total = above[j] + middle[j] + below[j] + shift[:, lo:hi]
                if stage == 1:
                    total = total + res_ref[0, i, :, lo:hi].astype(jnp.float32)
                rounded = total.astype(jnp.bfloat16)
                y_ref[0, i, :, lo:hi] = rounded
                if stage == 0:
                    mean, spread = row_moments(rounded.astype(jnp.float32))
                    m_ref[0, 0, 0, i:i + 1, lo:hi] = mean
                    m_ref[0, 1, 0, i:i + 1, lo:hi] = spread
        if stage == 1:
            @pl.when(scal[0] == 0)
            def _():
                keep_ref[...] = own_ref[...]

            @pl.when(scal[0] != 0)
            def _():
                keep_ref[...] = y_ref[...]
        carry_ref[:, 0:main] = p_ref[before, (block - 1) * columns:block * columns, 0:main]
        carry_ref[:, main:channels] = p_ref[before, (block - 1) * columns:block * columns, base:base + tail]


def conv(stage, sample, scal, source, top, bottom, stats, params, own, other, latents=None, out=None):
    rows, columns, channels = source.shape[1:]
    block = pick_block(rows)
    chunks = rows // block
    width = packed_width(channels)
    unit = -(-block // 2)
    tile = (1, block, columns, channels)
    lag = lambda c: jnp.maximum(c - 1, 0)
    ahead = lambda c: jnp.minimum(c, chunks - 1)
    full = lambda a: pl.BlockSpec(a.shape, lambda c, scal, n=a.ndim: (0,) * n)
    anywhere = pl.BlockSpec(memory_space=pl.ANY)
    if stage == 0:
        main_spec = pl.BlockSpec(tile, lambda c, scal: (scal[3] + sample, ahead(c), 0, 0))
    else:
        main_spec = pl.BlockSpec(tile, lambda c, scal: (0, ahead(c), 0, 0))
    args = [source, top, bottom, *stats, params, own, other]
    in_specs = [main_spec, full(top), full(bottom), *[
        pl.BlockSpec((1,) + s.shape[1:], lambda c, scal: ((sample if stage == 0 else 0), 0, 0, 0, 0)) for s in stats
    ], full(params), anywhere, anywhere]
    plain = jax.ShapeDtypeStruct((1, rows, columns, channels), jnp.bfloat16)
    plain_spec = pl.BlockSpec(tile, lambda c, scal: (0, lag(c), 0, 0))
    aliases = {}
    if stage == 0:
        out_shape = (plain, jax.ShapeDtypeStruct((1, 2, chunks, block, channels), jnp.float32))
        out_specs = (plain_spec, pl.BlockSpec((1, 2, 1, block, channels), lambda c, scal: (0, 0, lag(c), 0, 0)))
    else:
        placed = pl.BlockSpec(tile, lambda c, scal: (scal[3] + sample, lag(c), 0, 0))
        args += [latents, source]
        in_specs += [placed, plain_spec]
        if out is not None:
            args.append(out)
            in_specs.append(anywhere)
            aliases = {len(args): 0}
        out_shape = (jax.ShapeDtypeStruct(latents.shape, jnp.bfloat16), plain)
        out_specs = (placed, plain_spec)
    return pl.pallas_call(
        functools.partial(conv_kernel, stage, len(stats)),
        grid_spec=pltpu.PrefetchScalarGridSpec(
            num_scalar_prefetch=1,
            grid=(chunks + 1,),
            in_specs=in_specs,
            out_specs=out_specs,
            scratch_shapes=[
                pltpu.VMEM((width, width), jnp.bfloat16),
                pltpu.VMEM((block, columns + 16, channels), jnp.float32),
                pltpu.VMEM((unit * columns, width), jnp.bfloat16),
                pltpu.VMEM((unit * columns, width), jnp.bfloat16),
                pltpu.VMEM((2, block * columns, width), jnp.float32),
                pltpu.VMEM((columns, channels), jnp.float32),
                pltpu.VMEM((columns, channels), jnp.float32),
                pltpu.VMEM((8, channels), jnp.float32),
                pltpu.SemaphoreType.DMA((1,)),
            ],
        ),
        out_shape=out_shape,
        input_output_aliases=aliases,
        compiler_params=pltpu.CompilerParams(
            vmem_limit_bytes=VMEM_LIMIT, dimension_semantics=("arbitrary",)
        ),
        cost_estimate=pl.CostEstimate(
            flops=2 * rows * columns * width * width,
            bytes_accessed=4 * rows * columns * channels,
            transcendentals=rows * columns * channels,
        ),
        name=f"conv{stage}",
    )(scal, *args)


def place_kernel(scal, a_ref, b_ref, _, out_ref):
    @pl.when(scal[0] == 0)
    def _():
        out_ref[...] = a_ref[...]

    @pl.when(scal[0] != 0)
    def _():
        out_ref[...] = b_ref[...]


def place(sample, count, scal, when_first, when_second, out):
    rows, columns, channels = out.shape[1:]
    block = pick_block(rows)
    tile = (1, block, columns, channels)
    return pl.pallas_call(
        place_kernel,
        grid_spec=pltpu.PrefetchScalarGridSpec(
            num_scalar_prefetch=1,
            grid=(rows // block,),
            in_specs=[
                pl.BlockSpec(tile, lambda c, scal: (0, jnp.where(scal[0] == 0, c, 0), 0, 0)),
                pl.BlockSpec(tile, lambda c, scal: (0, jnp.where(scal[0] == 0, 0, c), 0, 0)),
                pl.BlockSpec(memory_space=pl.ANY),
            ],
            out_specs=pl.BlockSpec(tile, lambda c, scal: ((1 - scal[0]) * count + sample, c, 0, 0)),
        ),
        out_shape=jax.ShapeDtypeStruct(out.shape, out.dtype),
        input_output_aliases={3: 0},
        compiler_params=pltpu.CompilerParams(vmem_limit_bytes=VMEM_LIMIT),
        cost_estimate=pl.CostEstimate(flops=0, bytes_accessed=4 * rows * columns * channels, transcendentals=0),
        name="place",
    )(scal, when_first, when_second, out)


def everyones(value):
    size = lax.axis_size("space")
    if size > 4:
        gathered = lax.all_gather(value, "space", axis=0)
        return [gathered[i] for i in range(size)]
    found = [value]
    for hop in range(1, size):
        found.append(lax.ppermute(value, "space", [(i, (i + hop) % size) for i in range(size)]))
    return found


def edge_rows(last, first):
    size = lax.axis_size("space")
    up = [(i, i + 1) for i in range(size - 1)]
    return lax.ppermute(last, "space", up), lax.ppermute(first, "space", [(j, i) for i, j in up])


def on_device(latents, kernels, norm_gain, norm_bias, conv_bias):
    section = lax.axis_index("section")
    space, spaces = lax.axis_index("space"), lax.axis_size("space")
    samples = latents.shape[0]
    count = samples // lax.axis_size("section")
    scal = jnp.stack([section, (space > 0).astype(jnp.int32), (space < spaces - 1).astype(jnp.int32), section * count])
    scal = scal.astype(jnp.int32)

    swap = [(0, 1), (1, 0)]
    own_w = pack_weights(kernels[0])
    other_w = lax.ppermute(own_w, "section", swap)
    own_p = jnp.concatenate([norm_gain, norm_bias, conv_bias, jnp.zeros((5, norm_gain.shape[1]), jnp.float32)])
    other_p = lax.ppermute(own_p, "section", swap)
    params = [jnp.where(section == stage, own_p, other_p) for stage in range(2)]

    edges = [
        lax.dynamic_slice(latents, (section * count, row, 0, 0), (count, 1) + latents.shape[2:])[:, 0]
        for row in (latents.shape[1] - 1, 0)
    ]
    tops, bottoms = edge_rows(*edges)
    stats = everyones(moments(scal, latents, count))

    firsts, halos, first_stats, arrived = [], [], [], []
    for s in range(count):
        first, own_stats = conv(0, s, scal, latents, tops[s], bottoms[s], stats, params[0], own_w, other_w)
        firsts.append(first)
        first_stats.append(everyones(own_stats))
        halos.append(edge_rows(first[0, -1], first[0, 0]))
        arrived.append(lax.ppermute(first, "section", [(1, 0)]))
    out, sent = None, []
    for s in range(count):
        out, second = conv(
            1, s, scal, firsts[s], *halos[s], first_stats[s], params[1], own_w, other_w, latents, out
        )
        sent.append(lax.ppermute(second, "section", [(0, 1)]))
    for s in range(count):
        out = place(s, count, scal, arrived[s], sent[s], out)
    return out[None]


def solution(mesh):
    return jax.shard_map(
        on_device,
        mesh=mesh,
        in_specs=(
            P("dp", "space", None, None),
            P("section", None, None, None, None),
            P("section", None),
            P("section", None),
            P("section", None),
        ),
        out_specs=P("section", "dp", "space", None, None),
        check_vma=False,
    )
```

time: 427 us -> 172 us (0.40); the launches traced: 418 us -> 170 us
  local copies, waits for them, and re-layouts: 170 us -> 6.82 us
  Pallas kernels: 0 us -> 110 us
  other arithmetic: 96.9 us -> 1.35 us
  matrix products: 67 us -> 0 us
  blocking collectives: 59.3 us -> 0 us
  starting transfers between devices: 10.7 us -> 42.3 us
  between operations: 14.3 us -> 0.28 us
  waiting for transfers between devices: 0.03 us -> 8.86 us
    pallas_call x0 -> x8, Pallas kernels: none -> 110 us  [the longest x4 87.3 us: conv(): pl.pallas_call(functools.partial(conv_kernel, stage, len(stats)), grid_sp...]
    unnamed x29 -> x30, local copies, waits for them, and re-layouts: 82.2 us -> 2.12 us
    conv_general_dilated x2 -> x0, matrix products: 67 us -> none  [apply_layer(): lax.conv_general_dilated(normed, kernel, (1, 1), ((0, 0), (1, 1)), dimens...]
    psum x4 -> x0, blocking collectives: 38.7 us -> none  [the longest x2 19.5 us: group_moments(): totals = lax.psum(jnp.sum(values, axis=(1, 3)), 'space')]
    ppermute x4 -> x21, starting transfers between devices: 10.7 us -> 42.3 us  [the longest x9 17.8 us: everyones(): lax.ppermute(value, 'space', [(i, (i + hop) % size) for i in range(size)])]
    convert_element_type x9 -> x0, local copies, waits for them, and re-layouts: 31.3 us -> none  [the longest x2 18.3 us: apply_layer(): normed = jnp.where(outside, 0.0, activated).astype(jnp.bfloat16)]
    reduce_sum x8 -> x0, other arithmetic: 25.7 us -> none  [the longest x4 12.9 us: group_moments(): totals = lax.psum(jnp.sum(values, axis=(1, 3)), 'space')]
    convert_element_type x5 -> x0, other arithmetic: 25.5 us -> none  [the longest x2 25.5 us: apply_layer(): normed = jnp.where(outside, 0.0, activated).astype(jnp.bfloat16)]
  transfers between devices with their start and end apart: 5 -> 21, of which waited for: 0 -> 3; matrix products, arithmetic and copies ran while one was open for 22% -> 4% of each run, Pallas kernels for 0% -> 47%
where the time goes in v1:
time: 172 us; the launch traced here: 170 us
  Pallas kernels  110 us (64%)
  starting transfers between devices  42.3 us (25%)
  waiting for transfers between devices  8.86 us (5%)
  local copies, waits for them, and re-layouts  6.82 us (4%)
    pallas_call x4, Pallas kernels, conv(): pl.pallas_call(functools.partial(conv_kernel, stage, len(stats)), grid_sp...  87.3 us
    ppermute x9, starting transfers between devices, everyones(): lax.ppermute(value, 'space', [(i, (i + hop) % size) for i in range(size)])  17.8 us
    pallas_call x2, Pallas kernels, place(): pl.pallas_call(place_kernel, grid_spec=pltpu.PrefetchScalarGridSpec(num_s...  11.5 us
    ppermute x2, starting transfers between devices, on_device(): sent.append(lax.ppermute(second, 'section', [(0, 1)]))  11.5 us
    pallas_call x1, Pallas kernels, moments(): pl.pallas_call(moments_kernel, grid_spec=pltpu.PrefetchScalarGridSpec(num...  7.99 us
    ppermute x3, starting transfers between devices, edge_rows(): lax.ppermute(last, 'space', up)  5.86 us
    ppermute x3, waiting for transfers between devices, edge_rows(): lax.ppermute(last, 'space', up)  5.11 us
    ppermute x3, starting transfers between devices, edge_rows(): lax.ppermute(first, 'space', [(j, i) for i, j in up])  4.06 us
  transfers between devices with their start and end apart: 21, of which 3 were waited for; matrix products, arithmetic and copies ran while one was open for 4% of the time, Pallas kernels for 47%

profile of v1, /device:TPU:0, one launch (start us, length us, event | category | flops | bytes accessed | tf_op | source)
XLA Modules:
  0.0 170.0 jit_solution(16315847444144684907)
XLA Ops:
  0.0 3.6 %pack.1.refs_9_ = bf16[1024,1024]{1,0:T(8,128)(2,1)} custom-call(bf16[3,3,320,320]{3,2,1,0:T(8,128)(2,1)} %bitcast.26), custom_call_target="tpu_custom_call" | custom-call | bytes 6291456 | tf_op jit(solution)/shard_map/pack/pallas_call | solution.py:46
  5.2 1.3 collective-permute-start.1
  7.3 8.0 %moments.1.refs_4_ = f32[2,2,3,8,320]{4,3,2,1,0:T(8,128)} custom-call(s32[4]{0:T(128)} %pad_add_fusion.scal.refs_0_, bf16[4,24,192,320]{3,2,1,0:T(8,128)(2,1)} %refs_11_.3), custom_call_target="tpu_custom_call" | custom-call | bytes 5898240 | tf_op jit(solution)/shard_map/moments/pallas_call | solution.py:72
  15.3 3.6 %collective-permute-start.2 = (f32[2,2,3,8,320]{4,3,2,1,0:T(8,128)}, f32[2,2,3,8,320]{4,3,2,1,0:T(8,128)S(1)}, u32[]{:S(2)}, u32[]{:S(2)}) collective-permute-start(f32[2,2,3,8,320]{4,3,2,1,0:T(8,128)} %moments.1.refs_4_), channel_id=1, source_target_pairs={{0,1},{1,2},{2,3},{3,0},{4,5},{5,6},{6,7},{7,4},{8,9},{9,10},{10,1... | collective-permute-start | bytes 368648 | tf_op jit(solution)/shard_map/ppermute | solution.py:355
  18.9 1.8 %collective-permute-start.3 = (f32[2,2,3,8,320]{4,3,2,1,0:T(8,128)}, f32[2,2,3,8,320]{4,3,2,1,0:T(8,128)S(1)}, u32[]{:S(2)}, u32[]{:S(2)}) collective-permute-start(f32[2,2,3,8,320]{4,3,2,1,0:T(8,128)} %moments.1.refs_4_), channel_id=1, source_target_pairs={{0,2},{1,3},{2,0},{3,1},{4,6},{5,7},{6,4},{7,5},{8,10},{9,11},{10,... | collective-permute-start | bytes 368648 | tf_op jit(solution)/shard_map/ppermute | solution.py:355
  20.6 2.8 %collective-permute-start = (bf16[2,192,320]{2,1,0:T(8,128)(2,1)S(1)}, bf16[2,192,320]{2,1,0:T(8,128)(2,1)S(1)}, u32[]{:S(2)}, u32[]{:S(2)}) collective-permute-start(bf16[2,192,320]{2,1,0:T(8,128)(2,1)S(1)} %get-tuple-element.22), channel_id=1, source_target_pairs={{0,1},{1,2},{2,3},{4,5},{5,6},{6,7},{8,9},{9,10},{10,11},{12,13},{... | collective-permute-start | bytes 737288 | tf_op jit(solution)/shard_map/ppermute | solution.py:362
  25.7 5.1 %collective-permute-done = bf16[2,192,320]{2,1,0:T(8,128)(2,1)S(1)} collective-permute-done((bf16[2,192,320]{2,1,0:T(8,128)(2,1)S(1)}, bf16[2,192,320]{2,1,0:T(8,128)(2,1)S(1)}, u32[]{:S(2)}, u32[]{:S(2)}) %collective-permute-start) | collective-permute-done | bytes 245792 | tf_op jit(solution)/shard_map/ppermute | solution.py:362
  31.5 2.2 %collective-permute-done.3.refs_6_ = f32[2,2,3,8,320]{4,3,2,1,0:T(8,128)S(1)} collective-permute-done((f32[2,2,3,8,320]{4,3,2,1,0:T(8,128)}, f32[2,2,3,8,320]{4,3,2,1,0:T(8,128)S(1)}, u32[]{:S(2)}, u32[]{:S(2)}) %collective-permute-start.3) | collective-permute-done | bytes 122912 | tf_op jit(solution)/shard_map/ppermute | solution.py:355
  33.7 1.5 collective-permute-done.4.refs_7_
  36.6 21.4 %conv0.3 = (bf16[1,24,192,320]{3,2,1,0:T(8,128)(2,1)}, f32[1,2,3,8,320]{4,3,2,1,0:T(8,128)}) custom-call(s32[4]{0:T(128)} %pad_add_fusion.scal.refs_0_, bf16[4,24,192,320]{3,2,1,0:T(8,128)(2,1)} %refs_11_.3, bf16[192,320]{1,0:T(8,128)(2,1)} %get-tuple-element.29.refs_2_, bf16[192,320]{1,0:T(8,128)(2,1)} %get-tuple-element.27.refs_3_, ...), custom_call_target="tpu_custom_call" | custom-call | flops 9663676416 | bytes 5898240 | tf_op jit(solution)/shard_map/conv0/pallas_call | solution.py:281
  58.0 1.4 collective-permute-start.15
  59.7 2.1 %collective-permute-start.17 = (f32[1,2,3,8,320]{4,3,2,1,0:T(8,128)}, f32[1,2,3,8,320]{4,3,2,1,0:T(8,128)S(1)}, u32[]{:S(2)}, u32[]{:S(2)}) collective-permute-start(f32[1,2,3,8,320]{4,3,2,1,0:T(8,128)} %get-tuple-element.16.refs_4_), channel_id=1, source_target_pairs={{0,3},{1,0},{2,1},{3,2},{4,7},{5,4},{6,5},{7,6},{8,11},{9,8},{10,9... | collective-permute-start | bytes 184328 | tf_op jit(solution)/shard_map/ppermute | solution.py:355
  62.9 1.8 %collective-permute-start.13 = (bf16[192,320]{1,0:T(8,128)(2,1)S(1)}, bf16[192,320]{1,0:T(8,128)(2,1)S(1)}, u32[]{:S(2)}, u32[]{:S(2)}) collective-permute-start(bf16[192,320]{1,0:T(8,128)(2,1)S(1)} %get-tuple-element.24), channel_id=1, source_target_pairs={{0,1},{1,2},{2,3},{4,5},{5,6},{6,7},{8,9},{9,10},{10,11},{12,13},{... | collective-permute-start | bytes 368648 | tf_op jit(solution)/shard_map/ppermute | solution.py:362
  64.7 1.5 collective-permute-start.14
  66.2 21.4 %conv0.2 = (bf16[1,24,192,320]{3,2,1,0:T(8,128)(2,1)}, f32[1,2,3,8,320]{4,3,2,1,0:T(8,128)}) custom-call(s32[4]{0:T(128)} %pad_add_fusion.scal.refs_0_, bf16[4,24,192,320]{3,2,1,0:T(8,128)(2,1)} %refs_11_.3, bf16[192,320]{1,0:T(8,128)(2,1)} %get-tuple-element.30.refs_2_, bf16[192,320]{1,0:T(8,128)(2,1)} %get-tuple-element.28.refs_3_, ...), custom_call_target="tpu_custom_call" | custom-call | flops 9663676416 | bytes 5898240 | tf_op jit(solution)/shard_map/conv0/pallas_call | solution.py:281
  88.6 3.4 %collective-permute-start.10 = (f32[1,2,3,8,320]{4,3,2,1,0:T(8,128)}, f32[1,2,3,8,320]{4,3,2,1,0:T(8,128)}, u32[]{:S(2)}, u32[]{:S(2)}) collective-permute-start(f32[1,2,3,8,320]{4,3,2,1,0:T(8,128)} %get-tuple-element.14.refs_4_), channel_id=1, source_target_pairs={{0,1},{1,2},{2,3},{3,0},{4,5},{5,6},{6,7},{7,4},{8,9},{9,10},{10,1... | collective-permute-start | bytes 184328 | tf_op jit(solution)/shard_map/ppermute | solution.py:355
  92.0 1.5 collective-permute-start.11
  93.6 2.8 %collective-permute-start.12 = (f32[1,2,3,8,320]{4,3,2,1,0:T(8,128)}, f32[1,2,3,8,320]{4,3,2,1,0:T(8,128)}, u32[]{:S(2)}, u32[]{:S(2)}) collective-permute-start(f32[1,2,3,8,320]{4,3,2,1,0:T(8,128)} %get-tuple-element.14.refs_4_), channel_id=1, source_target_pairs={{0,3},{1,0},{2,1},{3,2},{4,7},{5,4},{6,5},{7,6},{8,11},{9,8},{10,9... | collective-permute-start | bytes 184328 | tf_op jit(solution)/shard_map/ppermute | solution.py:355
  99.1 22.3 %conv1.2 = (bf16[4,24,192,320]{3,2,1,0:T(8,128)(2,1)}, bf16[1,24,192,320]{3,2,1,0:T(8,128)(2,1)}) custom-call(s32[4]{0:T(128)} %pad_add_fusion.scal.refs_0_, bf16[1,24,192,320]{3,2,1,0:T(8,128)(2,1)} %get-tuple-element.15.refs_1_.refs_12_, bf16[192,320]{1,0:T(8,128)(2,1)} %copy-done.9, bf16[192,320]{1,0:T(8,128)(2,1)} %copy-done.11, ...), custom_call_target="tpu_custom_call" | custom-call | flops 9663676416 | bytes 5898240 | tf_op jit(solution)/shard_map/conv1/pallas_call | solution.py:281
  124.1 8.4 %collective-permute-start.20 = (bf16[1,24,192,320]{3,2,1,0:T(8,128)(2,1)}, bf16[1,24,192,320]{3,2,1,0:T(8,128)(2,1)}, u32[]{:S(2)}, u32[]{:S(2)}) collective-permute-start(bf16[1,24,192,320]{3,2,1,0:T(8,128)(2,1)} %get-tuple-element.19), channel_id=1, source_target_pairs={{0,4},{1,5},{2,6},{3,7},{8,12},{9,13},{10,14},{11,15},{16,20},{17,... | collective-permute-start | bytes 8847368 | tf_op jit(solution)/shard_map/ppermute | solution.py:399
  133.2 22.2 %conv1.3 = (bf16[4,24,192,320]{3,2,1,0:T(8,128)(2,1)}, bf16[1,24,192,320]{3,2,1,0:T(8,128)(2,1)}) custom-call(s32[4]{0:T(128)} %pad_add_fusion.scal.refs_0_, bf16[1,24,192,320]{3,2,1,0:T(8,128)(2,1)} %get-tuple-element.13.refs_1_.refs_12_, bf16[192,320]{1,0:T(8,128)(2,1)} %copy-done.2, bf16[192,320]{1,0:T(8,128)(2,1)} %copy-done.3, ...), custom_call_target="tpu_custom_call", output_to_operand_aliasing={{0}: (13, {})} | custom-call | flops 9663676416 | bytes 5898240 | tf_op jit(solution)/shard_map/conv1/pallas_call | solution.py:281
  155.4 3.1 %collective-permute-start.18 = (bf16[1,24,192,320]{3,2,1,0:T(8,128)(2,1)}, bf16[1,24,192,320]{3,2,1,0:T(8,128)(2,1)}, u32[]{:S(2)}, u32[]{:S(2)}) collective-permute-start(bf16[1,24,192,320]{3,2,1,0:T(8,128)(2,1)} %get-tuple-element.18), channel_id=1, source_target_pairs={{0,4},{1,5},{2,6},{3,7},{8,12},{9,13},{10,14},{11,15},{16,20},{17,... | collective-permute-start | bytes 8847368 | tf_op jit(solution)/shard_map/ppermute | solution.py:399
  158.5 5.7 %place.2._ = bf16[4,24,192,320]{3,2,1,0:T(8,128)(2,1)} custom-call(s32[4]{0:T(128)} %pad_add_fusion.scal.refs_0_, bf16[1,24,192,320]{3,2,1,0:T(8,128)(2,1)} %collective-permute-done.19.a_ref, bf16[1,24,192,320]{3,2,1,0:T(8,128)(2,1)} %collective-permute-done.20.b_ref, bf16[4,24,192,320]{3,2,1,0:T(8,128)(2,1)} %get-tuple-element.20._), custom_call_target="tpu_custom_call", output_to_operand_aliasing={{}: (3, {})} | custom-call | bytes 5898240 | tf_op jit(solution)/shard_map/place/pallas_call | solution.py:328
  164.3 5.7 %place.3 = bf16[4,24,192,320]{3,2,1,0:T(8,128)(2,1)} custom-call(s32[4]{0:T(128)} %pad_add_fusion.scal.refs_0_, bf16[1,24,192,320]{3,2,1,0:T(8,128)(2,1)} %collective-permute-done.7.a_ref, bf16[1,24,192,320]{3,2,1,0:T(8,128)(2,1)} %collective-permute-done.18.b_ref, bf16[4,24,192,320]{3,2,1,0:T(8,128)(2,1)} %place.2._), custom_call_target="tpu_custom_call", output_to_operand_aliasing={{}: (3, {})} | custom-call | bytes 5898240 | tf_op jit(solution)/shard_map/place/pallas_call | solution.py:328
  (66 shorter events, 15.0 us)
Async XLA Ops:
  3.6 31.7 %collective-permute-start.6 = (bf16[1024,1024]{1,0:T(8,128)(2,1)}, bf16[1024,1024]{1,0:T(8,128)(2,1)S(1)}, u32[]{:S(2)}, u32[]{:S(2)}) collective-permute-start(bf16[1024,1024]{1,0:T(8,128)(2,1)} %pack.1.refs_9_), channel_id=1, source_target_pairs={{0,4},{4,0},{1,5},{5,1},{2,6},{6,2},{3,7},{7,3},{8,12},{12,8},{9,1... | collective-permute-start | bytes 6291464 | tf_op jit(solution)/shard_map/ppermute | solution.py:375
  5.2 18.9 %collective-permute-start.1 = (bf16[2,192,320]{2,1,0:T(8,128)(2,1)S(1)}, bf16[2,192,320]{2,1,0:T(8,128)(2,1)S(1)}, u32[]{:S(2)}, u32[]{:S(2)}) collective-permute-start(bf16[2,192,320]{2,1,0:T(8,128)(2,1)S(1)} %get-tuple-element.21), channel_id=1, source_target_pairs={{1,0},{2,1},{3,2},{5,4},{6,5},{7,6},{9,8},{10,9},{11,10},{13,12},{... | collective-permute-start | bytes 737288 | tf_op jit(solution)/shard_map/ppermute | solution.py:362
  6.6 14.0 %collective-permute-start.5 = (f32[8,320]{1,0:T(8,128)S(1)}, f32[8,320]{1,0:T(8,128)S(1)}, u32[]{:S(2)}, u32[]{:S(2)}) collective-permute-start(f32[8,320]{1,0:T(8,128)S(1)} %maximum_maximum_fusion), channel_id=1, source_target_pairs={{0,4},{4,0},{1,5},{5,1},{2,6},{6,2},{3,7},{7,3},{8,12},{12,8},{9,1... | collective-permute-start | bytes 30728 | tf_op jit(solution)/shard_map/ppermute | solution.py:377
  15.3 16.3 %collective-permute-start.2 = (f32[2,2,3,8,320]{4,3,2,1,0:T(8,128)}, f32[2,2,3,8,320]{4,3,2,1,0:T(8,128)S(1)}, u32[]{:S(2)}, u32[]{:S(2)}) collective-permute-start(f32[2,2,3,8,320]{4,3,2,1,0:T(8,128)} %moments.1.refs_4_), channel_id=1, source_target_pairs={{0,1},{1,2},{2,3},{3,0},{4,5},{5,6},{6,7},{7,4},{8,9},{9,10},{10,1... | collective-permute-start | bytes 368648 | tf_op jit(solution)/shard_map/ppermute | solution.py:355
  18.9 14.8 %collective-permute-start.3 = (f32[2,2,3,8,320]{4,3,2,1,0:T(8,128)}, f32[2,2,3,8,320]{4,3,2,1,0:T(8,128)S(1)}, u32[]{:S(2)}, u32[]{:S(2)}) collective-permute-start(f32[2,2,3,8,320]{4,3,2,1,0:T(8,128)} %moments.1.refs_4_), channel_id=1, source_target_pairs={{0,2},{1,3},{2,0},{3,1},{4,6},{5,7},{6,4},{7,5},{8,10},{9,11},{10,... | collective-permute-start | bytes 368648 | tf_op jit(solution)/shard_map/ppermute | solution.py:355
  20.6 10.1 %collective-permute-start = (bf16[2,192,320]{2,1,0:T(8,128)(2,1)S(1)}, bf16[2,192,320]{2,1,0:T(8,128)(2,1)S(1)}, u32[]{:S(2)}, u32[]{:S(2)}) collective-permute-start(bf16[2,192,320]{2,1,0:T(8,128)(2,1)S(1)} %get-tuple-element.22), channel_id=1, source_target_pairs={{0,1},{1,2},{2,3},{4,5},{5,6},{6,7},{8,9},{9,10},{10,11},{12,13},{... | collective-permute-start | bytes 737288 | tf_op jit(solution)/shard_map/ppermute | solution.py:362
  24.1 11.1 %collective-permute-start.4 = (f32[2,2,3,8,320]{4,3,2,1,0:T(8,128)}, f32[2,2,3,8,320]{4,3,2,1,0:T(8,128)S(1)}, u32[]{:S(2)}, u32[]{:S(2)}) collective-permute-start(f32[2,2,3,8,320]{4,3,2,1,0:T(8,128)} %moments.1.refs_4_), channel_id=1, source_target_pairs={{0,3},{1,0},{2,1},{3,2},{4,7},{5,4},{6,5},{7,6},{8,11},{9,8},{10,9... | collective-permute-start | bytes 368648 | tf_op jit(solution)/shard_map/ppermute | solution.py:355
  58.0 30.6 %collective-permute-start.15 = (f32[1,2,3,8,320]{4,3,2,1,0:T(8,128)}, f32[1,2,3,8,320]{4,3,2,1,0:T(8,128)S(1)}, u32[]{:S(2)}, u32[]{:S(2)}) collective-permute-start(f32[1,2,3,8,320]{4,3,2,1,0:T(8,128)} %get-tuple-element.16.refs_4_), channel_id=1, source_target_pairs={{0,1},{1,2},{2,3},{3,0},{4,5},{5,6},{6,7},{7,4},{8,9},{9,10},{10,1... | collective-permute-start | bytes 184328 | tf_op jit(solution)/shard_map/ppermute | solution.py:355
  59.5 32.6 %collective-permute-start.16 = (f32[1,2,3,8,320]{4,3,2,1,0:T(8,128)}, f32[1,2,3,8,320]{4,3,2,1,0:T(8,128)S(1)}, u32[]{:S(2)}, u32[]{:S(2)}) collective-permute-start(f32[1,2,3,8,320]{4,3,2,1,0:T(8,128)} %get-tuple-element.16.refs_4_), channel_id=1, source_target_pairs={{0,2},{1,3},{2,0},{3,1},{4,6},{5,7},{6,4},{7,5},{8,10},{9,11},{10,... | collective-permute-start | bytes 184328 | tf_op jit(solution)/shard_map/ppermute | solution.py:355
  59.7 33.9 %collective-permute-start.17 = (f32[1,2,3,8,320]{4,3,2,1,0:T(8,128)}, f32[1,2,3,8,320]{4,3,2,1,0:T(8,128)S(1)}, u32[]{:S(2)}, u32[]{:S(2)}) collective-permute-start(f32[1,2,3,8,320]{4,3,2,1,0:T(8,128)} %get-tuple-element.16.refs_4_), channel_id=1, source_target_pairs={{0,3},{1,0},{2,1},{3,2},{4,7},{5,4},{6,5},{7,6},{8,11},{9,8},{10,9... | collective-permute-start | bytes 184328 | tf_op jit(solution)/shard_map/ppermute | solution.py:355
  62.9 33.5 %collective-permute-start.13 = (bf16[192,320]{1,0:T(8,128)(2,1)S(1)}, bf16[192,320]{1,0:T(8,128)(2,1)S(1)}, u32[]{:S(2)}, u32[]{:S(2)}) collective-permute-start(bf16[192,320]{1,0:T(8,128)(2,1)S(1)} %get-tuple-element.24), channel_id=1, source_target_pairs={{0,1},{1,2},{2,3},{4,5},{5,6},{6,7},{8,9},{9,10},{10,11},{12,13},{... | collective-permute-start | bytes 368648 | tf_op jit(solution)/shard_map/ppermute | solution.py:362
  64.7 33.0 %collective-permute-start.14 = (bf16[192,320]{1,0:T(8,128)(2,1)S(1)}, bf16[192,320]{1,0:T(8,128)(2,1)S(1)}, u32[]{:S(2)}, u32[]{:S(2)}) collective-permute-start(bf16[192,320]{1,0:T(8,128)(2,1)S(1)} %get-tuple-element.23), channel_id=1, source_target_pairs={{1,0},{2,1},{3,2},{5,4},{6,5},{7,6},{9,8},{10,9},{11,10},{13,12},{... | collective-permute-start | bytes 368648 | tf_op jit(solution)/shard_map/ppermute | solution.py:362
  88.6 10.4 %copy-start.12 = (f32[1,2,3,8,320]{4,3,2,1,0:T(8,128)}, f32[1,2,3,8,320]{4,3,2,1,0:T(8,128)S(1)}, u32[]{:S(2)}) copy-start(f32[1,2,3,8,320]{4,3,2,1,0:T(8,128)S(1)} %collective-permute-done.15.refs_5_) | copy-start | bytes 184324
  88.6 32.8 %collective-permute-start.10 = (f32[1,2,3,8,320]{4,3,2,1,0:T(8,128)}, f32[1,2,3,8,320]{4,3,2,1,0:T(8,128)}, u32[]{:S(2)}, u32[]{:S(2)}) collective-permute-start(f32[1,2,3,8,320]{4,3,2,1,0:T(8,128)} %get-tuple-element.14.refs_4_), channel_id=1, source_target_pairs={{0,1},{1,2},{2,3},{3,0},{4,5},{5,6},{6,7},{7,4},{8,9},{9,10},{10,1... | collective-permute-start | bytes 184328 | tf_op jit(solution)/shard_map/ppermute | solution.py:355
  92.0 7.0 %copy-start.13 = (f32[1,2,3,8,320]{4,3,2,1,0:T(8,128)}, f32[1,2,3,8,320]{4,3,2,1,0:T(8,128)S(1)}, u32[]{:S(2)}) copy-start(f32[1,2,3,8,320]{4,3,2,1,0:T(8,128)S(1)} %collective-permute-done.16.refs_6_) | copy-start | bytes 184324
  92.0 30.7 %collective-permute-start.11 = (f32[1,2,3,8,320]{4,3,2,1,0:T(8,128)}, f32[1,2,3,8,320]{4,3,2,1,0:T(8,128)}, u32[]{:S(2)}, u32[]{:S(2)}) collective-permute-start(f32[1,2,3,8,320]{4,3,2,1,0:T(8,128)} %get-tuple-element.14.refs_4_), channel_id=1, source_target_pairs={{0,2},{1,3},{2,0},{3,1},{4,6},{5,7},{6,4},{7,5},{8,10},{9,11},{10,... | collective-permute-start | bytes 184328 | tf_op jit(solution)/shard_map/ppermute | solution.py:355
  93.6 30.5 %collective-permute-start.12 = (f32[1,2,3,8,320]{4,3,2,1,0:T(8,128)}, f32[1,2,3,8,320]{4,3,2,1,0:T(8,128)}, u32[]{:S(2)}, u32[]{:S(2)}) collective-permute-start(f32[1,2,3,8,320]{4,3,2,1,0:T(8,128)} %get-tuple-element.14.refs_4_), channel_id=1, source_target_pairs={{0,3},{1,0},{2,1},{3,2},{4,7},{5,4},{6,5},{7,6},{8,11},{9,8},{10,9... | collective-permute-start | bytes 184328 | tf_op jit(solution)/shard_map/ppermute | solution.py:355
  96.4 36.1 %collective-permute-start.8 = (bf16[192,320]{1,0:T(8,128)(2,1)S(1)}, bf16[192,320]{1,0:T(8,128)(2,1)S(1)}, u32[]{:S(2)}, u32[]{:S(2)}) collective-permute-start(bf16[192,320]{1,0:T(8,128)(2,1)S(1)} %get-tuple-element.26), channel_id=1, source_target_pairs={{0,1},{1,2},{2,3},{4,5},{5,6},{6,7},{8,9},{9,10},{10,11},{12,13},{... | collective-permute-start | bytes 368648 | tf_op jit(solution)/shard_map/ppermute | solution.py:362
  97.8 34.8 %collective-permute-start.9 = (bf16[192,320]{1,0:T(8,128)(2,1)S(1)}, bf16[192,320]{1,0:T(8,128)(2,1)S(1)}, u32[]{:S(2)}, u32[]{:S(2)}) collective-permute-start(bf16[192,320]{1,0:T(8,128)(2,1)S(1)} %get-tuple-element.25), channel_id=1, source_target_pairs={{1,0},{2,1},{3,2},{5,4},{6,5},{7,6},{9,8},{10,9},{11,10},{13,12},{... | collective-permute-start | bytes 368648 | tf_op jit(solution)/shard_map/ppermute | solution.py:362
  99.1 23.7 %copy-start = (bf16[1,24,192,320]{3,2,1,0:T(8,128)(2,1)S(1)}, bf16[1,24,192,320]{3,2,1,0:T(8,128)(2,1)}, u32[]{:S(2)}) copy-start(bf16[1,24,192,320]{3,2,1,0:T(8,128)(2,1)} %get-tuple-element.13.refs_1_.refs_12_) | copy-start | bytes 8847364
  121.5 37.1 %collective-permute-start.19 = (bf16[1,24,192,320]{3,2,1,0:T(8,128)(2,1)}, bf16[1,24,192,320]{3,2,1,0:T(8,128)(2,1)}, u32[]{:S(2)}, u32[]{:S(2)}) collective-permute-start(bf16[1,24,192,320]{3,2,1,0:T(8,128)(2,1)} %get-tuple-element.15.refs_1_.refs_12_), channel_id=1, source_target_pairs={{4,0},{5,1},{6,2},{7,3},{12,8},{13,9},{14,10},{15,11},{20,16},{21,... | collective-permute-start | bytes 8847368 | tf_op jit(solution)/shard_map/ppermute | solution.py:393
  122.8 41.5 %collective-permute-start.7 = (bf16[1,24,192,320]{3,2,1,0:T(8,128)(2,1)S(1)}, bf16[1,24,192,320]{3,2,1,0:T(8,128)(2,1)}, u32[]{:S(2)}, u32[]{:S(2)}) collective-permute-start(bf16[1,24,192,320]{3,2,1,0:T(8,128)(2,1)S(1)} %copy-done), channel_id=1, source_target_pairs={{4,0},{5,1},{6,2},{7,3},{12,8},{13,9},{14,10},{15,11},{20,16},{21,... | collective-permute-start | bytes 8847368 | tf_op jit(solution)/shard_map/ppermute | solution.py:393
  124.1 34.4 %collective-permute-start.20 = (bf16[1,24,192,320]{3,2,1,0:T(8,128)(2,1)}, bf16[1,24,192,320]{3,2,1,0:T(8,128)(2,1)}, u32[]{:S(2)}, u32[]{:S(2)}) collective-permute-start(bf16[1,24,192,320]{3,2,1,0:T(8,128)(2,1)} %get-tuple-element.19), channel_id=1, source_target_pairs={{0,4},{1,5},{2,6},{3,7},{8,12},{9,13},{10,14},{11,15},{16,20},{17,... | collective-permute-start | bytes 8847368 | tf_op jit(solution)/shard_map/ppermute | solution.py:399
  155.4 8.8 %collective-permute-start.18 = (bf16[1,24,192,320]{3,2,1,0:T(8,128)(2,1)}, bf16[1,24,192,320]{3,2,1,0:T(8,128)(2,1)}, u32[]{:S(2)}, u32[]{:S(2)}) collective-permute-start(bf16[1,24,192,320]{3,2,1,0:T(8,128)(2,1)} %get-tuple-element.18), channel_id=1, source_target_pairs={{0,4},{1,5},{2,6},{3,7},{8,12},{9,13},{10,14},{11,15},{16,20},{17,... | collective-permute-start | bytes 8847368 | tf_op jit(solution)/shard_map/ppermute | solution.py:399
  (12 other events, 37.9 us)

commit v2 on v1

--- a/solution.py
+++ b/solution.py
@@ -15,6 +15,10 @@
 
 def pick_block(rows):
     return max(d for d in range(1, 9) if rows % d == 0)
+
+
+def conv_block(rows):
+    return max(d for d in range(1, 5) if rows % d == 0)
 
 
 def column_pieces(channels):
@@ -88,28 +92,28 @@
     )(scal, latents)
 
 
+def stat_rows(ref, columns, rows):
+    if len(ref.shape) == 2:
+        return [(ref[columns:columns + rows, :], ref[columns + rows:columns + 2 * rows, :])]
+    return [(ref[0, 0, j], ref[0, 1, j]) for j in range(ref.shape[2])]
+
+
 def conv_kernel(stage, parts, *refs):
     scal, x_ref, top_ref, bot_ref = refs[:4]
     stat_refs = refs[4:4 + parts]
     par_ref, wa_ref, wb_ref = refs[4 + parts:7 + parts]
     rest = refs[7 + parts:]
     if stage == 0:
-        y_ref, m_ref = rest[:2]
-        rest = rest[2:]
+        y_ref, m_ref, up_ref, down_ref = rest[:4]
     else:
-        if len(rest) > 13:
-            rest_in, rest = rest[:3], rest[3:]
-        else:
-            rest_in, rest = rest[:2], rest[2:]
-        res_ref, own_ref = rest_in[:2]
-        keep_ref, y_ref = rest[:2]
-        rest = rest[2:]
-    w_ref, act_ref, lhs_a, lhs_b, p_ref, carry_ref, next_ref, ab_ref, sem = rest
+        res_ref, own_ref = rest[:2]
+        keep_ref, y_ref = rest[-13:-11]
+    w_ref, act_ref, lhs_a, lhs_b, p_a, p_b, edge_ref, carry_ref, next_ref, ab_ref = rest[-11:-1]
+    sem = rest[-1]
     step, last = pl.program_id(0), pl.num_programs(0) - 1
     block, columns, channels = x_ref.shape[1:]
     main, tail, base = column_pieces(channels)
     width = w_ref.shape[0]
-    unit = -(-block // 2)
 
     @pl.when(step == 0)
     def _():
@@ -139,18 +143,18 @@
                 precision=lax.Precision.HIGHEST, preferred_element_type=jnp.float32,
             )[0:1]
 
-        chunks, rows_of = stat_refs[0].shape[-3:-1]
-        cells = parts * chunks * rows_of
+        rows = stat_refs[0].shape[2] * stat_refs[0].shape[3]
+        cells = parts * rows
         total = jnp.zeros((1, channels), jnp.float32)
         for ref in stat_refs:
-            for j in range(chunks):
-                total += jnp.sum(ref[0, 0, j], axis=0, keepdims=True)
+            for means, _ in stat_rows(ref, columns, rows):
+                total += jnp.sum(means, axis=0, keepdims=True)
         mean = over_groups(total) * (1.0 / (cells * per_group))
         spread = jnp.zeros((1, channels), jnp.float32)
         for ref in stat_refs:
-            for j in range(chunks):
-                away = ref[0, 0, j] - mean
-                spread += jnp.sum(away * away * float(columns) + ref[0, 1, j], axis=0, keepdims=True)
+            for means, squares in stat_rows(ref, columns, rows):
+                away = means - mean
+                spread += jnp.sum(away * away * float(columns) + squares, axis=0, keepdims=True)
         var = over_groups(spread) * (1.0 / (cells * per_group * columns))
         inv = lax.rsqrt(var + EPS)
         ab_ref[0:1, :] = mean
@@ -172,85 +176,112 @@
         lhs[rows, base:width] = jnp.concatenate(tails, axis=1).astype(jnp.bfloat16)
 
     def edge(ref, valid, tap, dst):
-        activate(ref[...], 0, lhs_a, 0, valid)
-        left = lhs_a[0:columns, :]
+        activate(ref[0:columns, :], 0, edge_ref, 0, valid)
+        left = edge_ref[...]
         dst[:, 0:main] = jnp.dot(left, w_ref[:, tap * main:(tap + 1) * main], preferred_element_type=jnp.float32)
         ends = jnp.dot(left, w_ref[:, base:width], preferred_element_type=jnp.float32)
         dst[:, main:channels] = ends[:, tap * tail:(tap + 1) * tail]
 
+    shift = par_ref[2:3, :]
+
+    def tap_of(p, i, tap):
+        rows = slice(i * columns, (i + 1) * columns)
+        return (
+            p[rows, tap * main:(tap + 1) * main],
+            p[rows, base + tap * tail:base + (tap + 1) * tail],
+        )
+
+    def whole(ref):
+        return ref[:, 0:main], ref[:, main:channels]
+
+    def combine(p, i):
+        chunk = jnp.maximum(step - 2, 0)
+        above = whole(carry_ref) if i == 0 else tap_of(p, i - 1, 0)
+        middle = tap_of(p, i, 1)
+        below = whole(next_ref) if i == block - 1 else tap_of(p, i + 1, 2)
+        for j, (lo, hi) in enumerate(((0, main), (main, channels))):
+            total = above[j] + middle[j] + below[j] + shift[:, lo:hi]
+            if stage == 1:
+                total = total + res_ref[0, i, :, lo:hi].astype(jnp.float32)
+            rounded = total.astype(jnp.bfloat16)
+            y_ref[0, i, :, lo:hi] = rounded
+            if stage == 0:
+                mean, spread = row_moments(rounded.astype(jnp.float32))
+                m_ref[0, 0, chunk, i:i + 1, lo:hi] = mean
+                m_ref[0, 1, chunk, i:i + 1, lo:hi] = spread
+            else:
+                keep_ref[0, i, :, lo:hi] = jnp.where(scal[0] == 0, own_ref[0, i, :, lo:hi], rounded)
+
+    def save_carry(p):
+        left, right = tap_of(p, block - 1, 0)
+        carry_ref[:, 0:main] = left
+        carry_ref[:, main:channels] = right
+
     @pl.when(step == 0)
     def _():
+        for i in range(block):
+            activate(x_ref[0, i], i, lhs_a, i)
+
+    @pl.when(step == 2)
+    def _():
         edge(top_ref, scal[1] == 1, 0, carry_ref)
 
+    def turn(lhs_now, lhs_next, p_now, p_before):
+        pieces = width // MAIN
+        for n in range(pieces):
+            cols = slice(n * MAIN, (n + 1) * MAIN)
+            p_now[:, cols] = jnp.dot(lhs_now[...], w_ref[:, cols], preferred_element_type=jnp.float32)
+            for i in range(n * block // pieces, (n + 1) * block // pieces):
+                activate(x_ref[0, i], i, lhs_next, i)
+                if i < block - 1:
+                    combine(p_before, i)
+        left, right = tap_of(p_now, 0, 2)
+        next_ref[:, 0:main] = left
+        next_ref[:, main:channels] = right
+        combine(p_before, block - 1)
+        save_carry(p_before)
+
+    middle_step = jnp.logical_and(step > 0, step < last)
+
+    @pl.when(jnp.logical_and(middle_step, step % 2 == 1))
+    def _():
+        turn(lhs_a, lhs_b, p_a, p_b)
+
+    @pl.when(jnp.logical_and(middle_step, step % 2 == 0))
+    def _():
+        turn(lhs_b, lhs_a, p_b, p_a)
+
+    if stage == 0:
+        @pl.when(step == 2)
+        def _():
+            down_ref[0:columns, :] = y_ref[0, 0].astype(jnp.float32)
+
     @pl.when(step == last)
     def _():
         edge(bot_ref, scal[2] == 1, 2, next_ref)
-
-    now = step % 2
-    before = 1 - now
-
-    @pl.when(step < last)
-    def _():
-        for u, lhs in ((0, lhs_a), (1, lhs_b)):
-            lo, hi = u * unit, min((u + 1) * unit, block)
-            if hi <= lo:
-                continue
-            for i in range(lo, hi):
-                activate(x_ref[0, i], i, lhs, i - lo)
-            p_ref[now, lo * columns:hi * columns, :] = jnp.dot(
-                lhs[0:(hi - lo) * columns, :], w_ref[...], preferred_element_type=jnp.float32
-            )
-        next_ref[:, 0:main] = p_ref[now, 0:columns, 2 * main:3 * main]
-        next_ref[:, main:channels] = p_ref[now, 0:columns, base + 2 * tail:base + 3 * tail]
-
-    @pl.when(step > 0)
-    def _():
-        shift = par_ref[2:3, :]
-
-        def tap_of(i, tap):
-            rows = slice(i * columns, (i + 1) * columns)
-            return (
-                p_ref[before, rows, tap * main:(tap + 1) * main],
-                p_ref[before, rows, base + tap * tail:base + (tap + 1) * tail],
-            )
-
-        def whole(ref):
-            return ref[:, 0:main], ref[:, main:channels]
-
-        for i in range(block):
-            above = whole(carry_ref) if i == 0 else tap_of(i - 1, 0)
-            middle = tap_of(i, 1)
-            below = whole(next_ref) if i == block - 1 else tap_of(i + 1, 2)
-            for j, (lo, hi) in enumerate(((0, main), (main, channels))):
-                total = above[j] + middle[j] + below[j] + shift[:, lo:hi]
-                if stage == 1:
-                    total = total + res_ref[0, i, :, lo:hi].astype(jnp.float32)
-                rounded = total.astype(jnp.bfloat16)
-                y_ref[0, i, :, lo:hi] = rounded
-                if stage == 0:
-                    mean, spread = row_moments(rounded.astype(jnp.float32))
-                    m_ref[0, 0, 0, i:i + 1, lo:hi] = mean
-                    m_ref[0, 1, 0, i:i + 1, lo:hi] = spread
-        if stage == 1:
-            @pl.when(scal[0] == 0)
+        for parity, p in ((1, p_a), (0, p_b)):
+            @pl.when((last - 1) % 2 == parity)
             def _():
-                keep_ref[...] = own_ref[...]
-
-            @pl.when(scal[0] != 0)
-            def _():
-                keep_ref[...] = y_ref[...]
-        carry_ref[:, 0:main] = p_ref[before, (block - 1) * columns:block * columns, 0:main]
-        carry_ref[:, main:channels] = p_ref[before, (block - 1) * columns:block * columns, base:base + tail]
+                for i in range(block):
+                    combine(p, i)
+        if stage == 0:
+            if m_ref.shape[2] == 1:
+                down_ref[0:columns, :] = y_ref[0, 0].astype(jnp.float32)
+            up_ref[0:columns, :] = y_ref[0, block - 1].astype(jnp.float32)
+            for j in range(m_ref.shape[2]):
+                for q in range(2):
+                    at = columns + (q * m_ref.shape[2] + j) * block
+                    for ref in (up_ref, down_ref):
+                        ref[at:at + block, :] = m_ref[0, q, j]
 
 
 def conv(stage, sample, scal, source, top, bottom, stats, params, own, other, latents=None, out=None):
     rows, columns, channels = source.shape[1:]
-    block = pick_block(rows)
+    block = conv_block(rows)
     chunks = rows // block
     width = packed_width(channels)
-    unit = -(-block // 2)
     tile = (1, block, columns, channels)
-    lag = lambda c: jnp.maximum(c - 1, 0)
+    lag = lambda c: jnp.clip(c - 2, 0, chunks - 1)
     ahead = lambda c: jnp.minimum(c, chunks - 1)
     full = lambda a: pl.BlockSpec(a.shape, lambda c, scal, n=a.ndim: (0,) * n)
     anywhere = pl.BlockSpec(memory_space=pl.ANY)
@@ -260,14 +291,18 @@
         main_spec = pl.BlockSpec(tile, lambda c, scal: (0, ahead(c), 0, 0))
     args = [source, top, bottom, *stats, params, own, other]
     in_specs = [main_spec, full(top), full(bottom), *[
-        pl.BlockSpec((1,) + s.shape[1:], lambda c, scal: ((sample if stage == 0 else 0), 0, 0, 0, 0)) for s in stats
+        full(s) if s.ndim == 2 else pl.BlockSpec(
+            (1,) + s.shape[1:], lambda c, scal: ((sample if stage == 0 else 0), 0, 0, 0, 0)
+        ) for s in stats
     ], full(params), anywhere, anywhere]
     plain = jax.ShapeDtypeStruct((1, rows, columns, channels), jnp.bfloat16)
     plain_spec = pl.BlockSpec(tile, lambda c, scal: (0, lag(c), 0, 0))
     aliases = {}
     if stage == 0:
-        out_shape = (plain, jax.ShapeDtypeStruct((1, 2, chunks, block, channels), jnp.float32))
-        out_specs = (plain_spec, pl.BlockSpec((1, 2, 1, block, channels), lambda c, scal: (0, 0, lag(c), 0, 0)))
+        moment = jax.ShapeDtypeStruct((1, 2, chunks, block, channels), jnp.float32)
+        message = jax.ShapeDtypeStruct((columns + 2 * rows, channels), jnp.float32)
+        out_shape = (plain, moment, message, message)
+        out_specs = (plain_spec, full(jnp.zeros(moment.shape)), full(jnp.zeros(message.shape)), full(jnp.zeros(message.shape)))
     else:
         placed = pl.BlockSpec(tile, lambda c, scal: (scal[3] + sample, lag(c), 0, 0))
         args += [latents, source]
@@ -282,15 +317,17 @@
         functools.partial(conv_kernel, stage, len(stats)),
         grid_spec=pltpu.PrefetchScalarGridSpec(
             num_scalar_prefetch=1,
-            grid=(chunks + 1,),
+            grid=(chunks + 2,),
             in_specs=in_specs,
             out_specs=out_specs,
             scratch_shapes=[
                 pltpu.VMEM((width, width), jnp.bfloat16),
                 pltpu.VMEM((block, columns + 16, channels), jnp.float32),
-                pltpu.VMEM((unit * columns, width), jnp.bfloat16),
-                pltpu.VMEM((unit * columns, width), jnp.bfloat16),
-                pltpu.VMEM((2, block * columns, width), jnp.float32),
+                pltpu.VMEM((block * columns, width), jnp.bfloat16),
+                pltpu.VMEM((block * columns, width), jnp.bfloat16),
+                pltpu.VMEM((block * columns, width), jnp.float32),
+                pltpu.VMEM((block * columns, width), jnp.float32),
+                pltpu.VMEM((columns, width), jnp.bfloat16),
                 pltpu.VMEM((columns, channels), jnp.float32),
                 pltpu.VMEM((columns, channels), jnp.float32),
                 pltpu.VMEM((8, channels), jnp.float32),
@@ -386,10 +423,20 @@
 
     firsts, halos, first_stats, arrived = [], [], [], []
     for s in range(count):
-        first, own_stats = conv(0, s, scal, latents, tops[s], bottoms[s], stats, params[0], own_w, other_w)
+        first, own_stats, up, down = conv(
+            0, s, scal, latents, tops[s], bottoms[s], stats, params[0], own_w, other_w
+        )
         firsts.append(first)
-        first_stats.append(everyones(own_stats))
-        halos.append(edge_rows(first[0, -1], first[0, 0]))
+        if 3 <= spaces <= 4:
+            ring = lambda hop: [(i, (i + hop) % spaces) for i in range(spaces)]
+            above, below = (lax.ppermute(up, "space", ring(1)), lax.ppermute(down, "space", ring(spaces - 1)))
+            others = [lax.ppermute(own_stats, "space", ring(hop)) for hop in range(2, spaces - 1)]
+            first_stats.append([own_stats, above, below, *others])
+            halos.append((above, below))
+        else:
+            first_stats.append(everyones(own_stats))
+            columns = latents.shape[2]
+            halos.append(edge_rows(up[0:columns], down[0:columns]))
         arrived.append(lax.ppermute(first, "section", [(1, 0)]))
     out, sent = None, []
     for s in range(count):

time: 172 us -> 169 us (0.983)
  starting transfers between devices: 42.3 us -> 31.5 us
  Pallas kernels: 110 us -> 119 us
    ppermute x9 -> x3, starting transfers between devices: 17.8 us -> 6.19 us  [everyones(): lax.ppermute(value, 'space', [(i, (i + hop) % size) for i in range(size)])]
    pallas_call x4, Pallas kernels: 87.3 us -> 95.5 us  [conv(): pl.pallas_call(functools.partial(conv_kernel, stage, len(stats)), grid_sp...]
    ppermute x0 -> x6, starting transfers between devices: none -> 7.96 us  [the longest x2 4.43 us: on_device(): lax.ppermute(down, 'space', ring(spaces - 1))]
    ppermute x3 -> x1, starting transfers between devices: 5.86 us -> 2.77 us  [edge_rows(): lax.ppermute(last, 'space', up)]
    ppermute x3 -> x1, starting transfers between devices: 4.06 us -> 1.29 us  [edge_rows(): lax.ppermute(first, 'space', [(j, i) for i, j in up])]
    unnamed x30 -> x26, local copies, waits for them, and re-layouts: 2.12 us -> 4.64 us
    squeeze x2 -> x0, local copies, waits for them, and re-layouts: 2.02 us -> none  [on_device(): halos.append(edge_rows(first[0, -1], first[0, 0]))]
    ppermute x9 -> x3, waiting for transfers between devices: 3.72 us -> 3.67 us  [everyones(): lax.ppermute(value, 'space', [(i, (i + hop) % size) for i in range(size)])]
  transfers between devices with their start and end apart: 21 -> 17, of which waited for: 3 -> 3; matrix products, arithmetic and copies ran while one was open for 4% -> 2% of each run, Pallas kernels for 47% -> 51%
where the time goes in v2:
time: 169 us; the launch traced here: 168 us
  Pallas kernels  119 us (70%)
  starting transfers between devices  31.5 us (19%)
  waiting for transfers between devices  8.82 us (5%)
  local copies, waits for them, and re-layouts  7.34 us (4%)
    pallas_call x4, Pallas kernels, conv(): pl.pallas_call(functools.partial(conv_kernel, stage, len(stats)), grid_sp...  95.5 us
    pallas_call x2, Pallas kernels, place(): pl.pallas_call(place_kernel, grid_spec=pltpu.PrefetchScalarGridSpec(num_s...  11.5 us
    ppermute x2, starting transfers between devices, on_device(): sent.append(lax.ppermute(second, 'section', [(0, 1)]))  10 us
    pallas_call x1, Pallas kernels, moments(): pl.pallas_call(moments_kernel, grid_spec=pltpu.PrefetchScalarGridSpec(num...  8 us
    ppermute x3, starting transfers between devices, everyones(): lax.ppermute(value, 'space', [(i, (i + hop) % size) for i in range(size)])  6.19 us
    ppermute x1, waiting for transfers between devices, edge_rows(): lax.ppermute(last, 'space', up)  5.11 us
    unnamed x26, local copies, waits for them, and re-layouts  4.64 us
    ppermute x2, starting transfers between devices, on_device(): lax.ppermute(down, 'space', ring(spaces - 1))  4.43 us
  transfers between devices with their start and end apart: 17, of which 3 were waited for; matrix products, arithmetic and copies ran while one was open for 2% of the time, Pallas kernels for 51%

profile of v2, /device:TPU:0, one launch (start us, length us, event | category | flops | bytes accessed | tf_op | source)
XLA Modules:
  0.0 167.8 jit_solution(9107666392658268684)
XLA Ops:
  0.0 3.5 %pack.1.refs_9_ = bf16[1024,1024]{1,0:T(8,128)(2,1)} custom-call(bf16[3,3,320,320]{3,2,1,0:T(8,128)(2,1)} %bitcast.18), custom_call_target="tpu_custom_call" | custom-call | bytes 6291456 | tf_op jit(solution)/shard_map/pack/pallas_call | solution.py:50
  5.1 1.3 collective-permute-start.1
  7.3 8.0 %moments.1.refs_4_ = f32[2,2,3,8,320]{4,3,2,1,0:T(8,128)} custom-call(s32[4]{0:T(128)} %pad_add_fusion.scal.refs_0_, bf16[4,24,192,320]{3,2,1,0:T(8,128)(2,1)} %refs_11_.3), custom_call_target="tpu_custom_call" | custom-call | bytes 5898240 | tf_op jit(solution)/shard_map/moments/pallas_call | solution.py:76
  15.3 3.6 %collective-permute-start.2 = (f32[2,2,3,8,320]{4,3,2,1,0:T(8,128)}, f32[2,2,3,8,320]{4,3,2,1,0:T(8,128)S(1)}, u32[]{:S(2)}, u32[]{:S(2)}) collective-permute-start(f32[2,2,3,8,320]{4,3,2,1,0:T(8,128)} %moments.1.refs_4_), channel_id=1, source_target_pairs={{0,1},{1,2},{2,3},{3,0},{4,5},{5,6},{6,7},{7,4},{8,9},{9,10},{10,1... | collective-permute-start | bytes 368648 | tf_op jit(solution)/shard_map/ppermute | solution.py:392
  18.9 1.8 %collective-permute-start.3 = (f32[2,2,3,8,320]{4,3,2,1,0:T(8,128)}, f32[2,2,3,8,320]{4,3,2,1,0:T(8,128)S(1)}, u32[]{:S(2)}, u32[]{:S(2)}) collective-permute-start(f32[2,2,3,8,320]{4,3,2,1,0:T(8,128)} %moments.1.refs_4_), channel_id=1, source_target_pairs={{0,2},{1,3},{2,0},{3,1},{4,6},{5,7},{6,4},{7,5},{8,10},{9,11},{10,... | collective-permute-start | bytes 368648 | tf_op jit(solution)/shard_map/ppermute | solution.py:392
  20.7 2.8 %collective-permute-start = (bf16[2,192,320]{2,1,0:T(8,128)(2,1)S(1)}, bf16[2,192,320]{2,1,0:T(8,128)(2,1)S(1)}, u32[]{:S(2)}, u32[]{:S(2)}) collective-permute-start(bf16[2,192,320]{2,1,0:T(8,128)(2,1)S(1)} %get-tuple-element.30), channel_id=1, source_target_pairs={{0,1},{1,2},{2,3},{4,5},{5,6},{6,7},{8,9},{9,10},{10,11},{12,13},{... | collective-permute-start | bytes 737288 | tf_op jit(solution)/shard_map/ppermute | solution.py:399
  25.7 5.1 %collective-permute-done = bf16[2,192,320]{2,1,0:T(8,128)(2,1)S(1)} collective-permute-done((bf16[2,192,320]{2,1,0:T(8,128)(2,1)S(1)}, bf16[2,192,320]{2,1,0:T(8,128)(2,1)S(1)}, u32[]{:S(2)}, u32[]{:S(2)}) %collective-permute-start) | collective-permute-done | bytes 245792 | tf_op jit(solution)/shard_map/ppermute | solution.py:399
  31.6 2.1 %collective-permute-done.3.refs_6_ = f32[2,2,3,8,320]{4,3,2,1,0:T(8,128)S(1)} collective-permute-done((f32[2,2,3,8,320]{4,3,2,1,0:T(8,128)}, f32[2,2,3,8,320]{4,3,2,1,0:T(8,128)S(1)}, u32[]{:S(2)}, u32[]{:S(2)}) %collective-permute-start.3) | collective-permute-done | bytes 122912 | tf_op jit(solution)/shard_map/ppermute | solution.py:392
  33.7 1.5 collective-permute-done.4.refs_7_
  36.7 23.7 %conv0.3 = (bf16[1,24,192,320]{3,2,1,0:T(8,128)(2,1)}, f32[1,2,6,4,320]{4,3,2,1,0:T(4,128)}, f32[240,320]{1,0:T(8,128)}, f32[240,320]{1,0:T(8,128)}) custom-call(s32[4]{0:T(128)} %pad_add_fusion.scal.refs_0_, bf16[4,24,192,320]{3,2,1,0:T(8,128)(2,1)} %refs_11_.3, bf16[192,320]{1,0:T(8,128)(2,1)} %get-tuple-element.33.refs_2_, ...), custom_call_target="tpu_custom_call" | custom-call | flops 9663676416 | bytes 5898240 | tf_op jit(solution)/shard_map/conv0/pallas_call | solution.py:316
  60.4 1.5 collective-permute-start.11
  61.8 1.5 collective-permute-start.12
  64.3 23.7 %conv0.2 = (bf16[1,24,192,320]{3,2,1,0:T(8,128)(2,1)}, f32[1,2,6,4,320]{4,3,2,1,0:T(4,128)}, f32[240,320]{1,0:T(8,128)}, f32[240,320]{1,0:T(8,128)}) custom-call(s32[4]{0:T(128)} %pad_add_fusion.scal.refs_0_, bf16[4,24,192,320]{3,2,1,0:T(8,128)(2,1)} %refs_11_.3, bf16[192,320]{1,0:T(8,128)(2,1)} %get-tuple-element.34.refs_2_, ...), custom_call_target="tpu_custom_call" | custom-call | flops 9663676416 | bytes 5898240 | tf_op jit(solution)/shard_map/conv0/pallas_call | solution.py:316
  88.1 2.9 %collective-permute-start.9 = (f32[240,320]{1,0:T(8,128)}, f32[240,320]{1,0:T(8,128)}, u32[]{:S(2)}, u32[]{:S(2)}) collective-permute-start(f32[240,320]{1,0:T(8,128)} %get-tuple-element.19), channel_id=1, source_target_pairs={{0,3},{1,0},{2,1},{3,2},{4,7},{5,4},{6,5},{7,6},{8,11},{9,8},{10,9... | collective-permute-start | bytes 921608 | tf_op jit(solution)/shard_map/ppermute | solution.py:432
  91.0 1.1 collective-permute-start.10
  92.1 1.3 collective-permute-start.15
  94.1 1.5 collective-permute-start.7
  95.7 24.1 %conv1.2 = (bf16[4,24,192,320]{3,2,1,0:T(8,128)(2,1)}, bf16[1,24,192,320]{3,2,1,0:T(8,128)(2,1)}) custom-call(s32[4]{0:T(128)} %pad_add_fusion.scal.refs_0_, bf16[1,24,192,320]{3,2,1,0:T(8,128)(2,1)} %get-tuple-element.21.refs_1_.refs_12_, f32[240,320]{1,0:T(8,128)} %copy-done.7, f32[240,320]{1,0:T(8,128)} %copy-done.8, ...), custom_call_target="tpu_custom_call" | custom-call | flops 9663676416 | bytes 5898240 | tf_op jit(solution)/shard_map/conv1/pallas_call | solution.py:316
  119.8 6.9 %collective-permute-start.16 = (bf16[1,24,192,320]{3,2,1,0:T(8,128)(2,1)}, bf16[1,24,192,320]{3,2,1,0:T(8,128)(2,1)}, u32[]{:S(2)}, u32[]{:S(2)}) collective-permute-start(bf16[1,24,192,320]{3,2,1,0:T(8,128)(2,1)} %get-tuple-element.27), channel_id=1, source_target_pairs={{0,4},{1,5},{2,6},{3,7},{8,12},{9,13},{10,14},{11,15},{16,20},{17,... | collective-permute-start | bytes 8847368 | tf_op jit(solution)/shard_map/ppermute | solution.py:446
  127.4 24.0 %conv1.3 = (bf16[4,24,192,320]{3,2,1,0:T(8,128)(2,1)}, bf16[1,24,192,320]{3,2,1,0:T(8,128)(2,1)}) custom-call(s32[4]{0:T(128)} %pad_add_fusion.scal.refs_0_, bf16[1,24,192,320]{3,2,1,0:T(8,128)(2,1)} %get-tuple-element.17.refs_1_.refs_12_, f32[240,320]{1,0:T(8,128)} %copy-done.2, ...), custom_call_target="tpu_custom_call", output_to_operand_aliasing={{0}: (13, {})} | custom-call | flops 9663676416 | bytes 5898240 | tf_op jit(solution)/shard_map/conv1/pallas_call | solution.py:316
  151.5 3.1 %collective-permute-start.14 = (bf16[1,24,192,320]{3,2,1,0:T(8,128)(2,1)}, bf16[1,24,192,320]{3,2,1,0:T(8,128)(2,1)}, u32[]{:S(2)}, u32[]{:S(2)}) collective-permute-start(bf16[1,24,192,320]{3,2,1,0:T(8,128)(2,1)} %get-tuple-element.26), channel_id=1, source_target_pairs={{0,4},{1,5},{2,6},{3,7},{8,12},{9,13},{10,14},{11,15},{16,20},{17,... | collective-permute-start | bytes 8847368 | tf_op jit(solution)/shard_map/ppermute | solution.py:446
  154.6 5.7 %place.2._ = bf16[4,24,192,320]{3,2,1,0:T(8,128)(2,1)} custom-call(s32[4]{0:T(128)} %pad_add_fusion.scal.refs_0_, bf16[1,24,192,320]{3,2,1,0:T(8,128)(2,1)} %collective-permute-done.15.a_ref, bf16[1,24,192,320]{3,2,1,0:T(8,128)(2,1)} %collective-permute-done.16.b_ref, bf16[4,24,192,320]{3,2,1,0:T(8,128)(2,1)} %get-tuple-element.28._), custom_call_target="tpu_custom_call", output_to_operand_aliasing={{}: (3, {})} | custom-call | bytes 5898240 | tf_op jit(solution)/shard_map/place/pallas_call | solution.py:365
  160.3 1.7 %copy-done = bf16[1,24,192,320]{3,2,1,0:T(8,128)(2,1)} copy-done((bf16[1,24,192,320]{3,2,1,0:T(8,128)(2,1)}, bf16[1,24,192,320]{3,2,1,0:T(8,128)(2,1)S(1)}, u32[]{:S(2)}) %copy-start) | copy-done | bytes 2949144
  162.1 5.7 %place.3 = bf16[4,24,192,320]{3,2,1,0:T(8,128)(2,1)} custom-call(s32[4]{0:T(128)} %pad_add_fusion.scal.refs_0_, bf16[1,24,192,320]{3,2,1,0:T(8,128)(2,1)} %copy-done, bf16[1,24,192,320]{3,2,1,0:T(8,128)(2,1)} %collective-permute-done.14.b_ref, bf16[4,24,192,320]{3,2,1,0:T(8,128)(2,1)} %place.2._), custom_call_target="tpu_custom_call", output_to_operand_aliasing={{}: (3, {})} | custom-call | bytes 5898240 | tf_op jit(solution)/shard_map/place/pallas_call | solution.py:365
  (52 shorter events, 9.4 us)
Async XLA Ops:
  0.0 6.5 %copy-start.6 = (f32[1,320]{1,0:T(1,128)S(1)}, f32[1,320]{1,0:T(1,128)}, u32[]{:S(2)}) copy-start(f32[1,320]{1,0:T(1,128)} %param.7) | copy-start | bytes 3844
  0.0 6.5 %copy-start.5 = (f32[1,320]{1,0:T(1,128)S(1)}, f32[1,320]{1,0:T(1,128)}, u32[]{:S(2)}) copy-start(f32[1,320]{1,0:T(1,128)} %param.8) | copy-start | bytes 3844
  0.0 6.5 %copy-start.4 = (f32[1,320]{1,0:T(1,128)S(1)}, f32[1,320]{1,0:T(1,128)}, u32[]{:S(2)}) copy-start(f32[1,320]{1,0:T(1,128)} %param.9) | copy-start | bytes 3844
  3.5 31.7 %collective-permute-start.6 = (bf16[1024,1024]{1,0:T(8,128)(2,1)}, bf16[1024,1024]{1,0:T(8,128)(2,1)S(1)}, u32[]{:S(2)}, u32[]{:S(2)}) collective-permute-start(bf16[1024,1024]{1,0:T(8,128)(2,1)} %pack.1.refs_9_), channel_id=1, source_target_pairs={{0,4},{4,0},{1,5},{5,1},{2,6},{6,2},{3,7},{7,3},{8,12},{12,8},{9,1... | collective-permute-start | bytes 6291464 | tf_op jit(solution)/shard_map/ppermute | solution.py:412
  5.1 19.0 %collective-permute-start.1 = (bf16[2,192,320]{2,1,0:T(8,128)(2,1)S(1)}, bf16[2,192,320]{2,1,0:T(8,128)(2,1)S(1)}, u32[]{:S(2)}, u32[]{:S(2)}) collective-permute-start(bf16[2,192,320]{2,1,0:T(8,128)(2,1)S(1)} %get-tuple-element.29), channel_id=1, source_target_pairs={{1,0},{2,1},{3,2},{5,4},{6,5},{7,6},{9,8},{10,9},{11,10},{13,12},{... | collective-permute-start | bytes 737288 | tf_op jit(solution)/shard_map/ppermute | solution.py:399
  6.6 14.1 %collective-permute-start.5 = (f32[8,320]{1,0:T(8,128)S(1)}, f32[8,320]{1,0:T(8,128)S(1)}, u32[]{:S(2)}, u32[]{:S(2)}) collective-permute-start(f32[8,320]{1,0:T(8,128)S(1)} %maximum_maximum_fusion), channel_id=1, source_target_pairs={{0,4},{4,0},{1,5},{5,1},{2,6},{6,2},{3,7},{7,3},{8,12},{12,8},{9,1... | collective-permute-start | bytes 30728 | tf_op jit(solution)/shard_map/ppermute | solution.py:414
  15.3 16.3 %collective-permute-start.2 = (f32[2,2,3,8,320]{4,3,2,1,0:T(8,128)}, f32[2,2,3,8,320]{4,3,2,1,0:T(8,128)S(1)}, u32[]{:S(2)}, u32[]{:S(2)}) collective-permute-start(f32[2,2,3,8,320]{4,3,2,1,0:T(8,128)} %moments.1.refs_4_), channel_id=1, source_target_pairs={{0,1},{1,2},{2,3},{3,0},{4,5},{5,6},{6,7},{7,4},{8,9},{9,10},{10,1... | collective-permute-start | bytes 368648 | tf_op jit(solution)/shard_map/ppermute | solution.py:392
  18.9 14.8 %collective-permute-start.3 = (f32[2,2,3,8,320]{4,3,2,1,0:T(8,128)}, f32[2,2,3,8,320]{4,3,2,1,0:T(8,128)S(1)}, u32[]{:S(2)}, u32[]{:S(2)}) collective-permute-start(f32[2,2,3,8,320]{4,3,2,1,0:T(8,128)} %moments.1.refs_4_), channel_id=1, source_target_pairs={{0,2},{1,3},{2,0},{3,1},{4,6},{5,7},{6,4},{7,5},{8,10},{9,11},{10,... | collective-permute-start | bytes 368648 | tf_op jit(solution)/shard_map/ppermute | solution.py:392
  20.7 10.1 %collective-permute-start = (bf16[2,192,320]{2,1,0:T(8,128)(2,1)S(1)}, bf16[2,192,320]{2,1,0:T(8,128)(2,1)S(1)}, u32[]{:S(2)}, u32[]{:S(2)}) collective-permute-start(bf16[2,192,320]{2,1,0:T(8,128)(2,1)S(1)} %get-tuple-element.30), channel_id=1, source_target_pairs={{0,1},{1,2},{2,3},{4,5},{5,6},{6,7},{8,9},{9,10},{10,11},{12,13},{... | collective-permute-start | bytes 737288 | tf_op jit(solution)/shard_map/ppermute | solution.py:399
  24.1 11.1 %collective-permute-start.4 = (f32[2,2,3,8,320]{4,3,2,1,0:T(8,128)}, f32[2,2,3,8,320]{4,3,2,1,0:T(8,128)S(1)}, u32[]{:S(2)}, u32[]{:S(2)}) collective-permute-start(f32[2,2,3,8,320]{4,3,2,1,0:T(8,128)} %moments.1.refs_4_), channel_id=1, source_target_pairs={{0,3},{1,0},{2,1},{3,2},{4,7},{5,4},{6,5},{7,6},{8,11},{9,8},{10,9... | collective-permute-start | bytes 368648 | tf_op jit(solution)/shard_map/ppermute | solution.py:392
  31.6 3.7 %copy-start.9 = (f32[2,2,3,8,320]{4,3,2,1,0:T(8,128)}, f32[2,2,3,8,320]{4,3,2,1,0:T(8,128)S(1)}, u32[]{:S(2)}) copy-start(f32[2,2,3,8,320]{4,3,2,1,0:T(8,128)S(1)} %collective-permute-done.2.refs_5_) | copy-start | bytes 368644
  60.4 31.7 %collective-permute-start.11 = (f32[240,320]{1,0:T(8,128)}, f32[240,320]{1,0:T(8,128)S(1)}, u32[]{:S(2)}, u32[]{:S(2)}) collective-permute-start(f32[240,320]{1,0:T(8,128)} %get-tuple-element.22), channel_id=1, source_target_pairs={{0,1},{1,2},{2,3},{3,0},{4,5},{5,6},{6,7},{7,4},{8,9},{9,10},{10,1... | collective-permute-start | bytes 921608 | tf_op jit(solution)/shard_map/ppermute | solution.py:432
  61.8 31.5 %collective-permute-start.12 = (f32[240,320]{1,0:T(8,128)}, f32[240,320]{1,0:T(8,128)S(1)}, u32[]{:S(2)}, u32[]{:S(2)}) collective-permute-start(f32[240,320]{1,0:T(8,128)} %get-tuple-element.23), channel_id=1, source_target_pairs={{0,3},{1,0},{2,1},{3,2},{4,7},{5,4},{6,5},{7,6},{8,11},{9,8},{10,9... | collective-permute-start | bytes 921608 | tf_op jit(solution)/shard_map/ppermute | solution.py:432
  63.4 27.6 %collective-permute-start.13 = (f32[1,2,6,4,320]{4,3,2,1,0:T(4,128)}, f32[1,2,6,4,320]{4,3,2,1,0:T(4,128)S(1)}, u32[]{:S(2)}, u32[]{:S(2)}) collective-permute-start(f32[1,2,6,4,320]{4,3,2,1,0:T(4,128)} %get-tuple-element.24.refs_4_), channel_id=1, source_target_pairs={{0,2},{1,3},{2,0},{3,1},{4,6},{5,7},{6,4},{7,5},{8,10},{9,11},{10,... | collective-permute-start | bytes 184328 | tf_op jit(solution)/shard_map/ppermute | solution.py:433
  88.0 38.7 %collective-permute-start.8 = (f32[240,320]{1,0:T(8,128)}, f32[240,320]{1,0:T(8,128)S(1)}, u32[]{:S(2)}, u32[]{:S(2)}) collective-permute-start(f32[240,320]{1,0:T(8,128)} %get-tuple-element.18), channel_id=1, source_target_pairs={{0,1},{1,2},{2,3},{3,0},{4,5},{5,6},{6,7},{7,4},{8,9},{9,10},{10,1... | collective-permute-start | bytes 921608 | tf_op jit(solution)/shard_map/ppermute | solution.py:432
  88.1 38.7 %collective-permute-start.9 = (f32[240,320]{1,0:T(8,128)}, f32[240,320]{1,0:T(8,128)}, u32[]{:S(2)}, u32[]{:S(2)}) collective-permute-start(f32[240,320]{1,0:T(8,128)} %get-tuple-element.19), channel_id=1, source_target_pairs={{0,3},{1,0},{2,1},{3,2},{4,7},{5,4},{6,5},{7,6},{8,11},{9,8},{10,9... | collective-permute-start | bytes 921608 | tf_op jit(solution)/shard_map/ppermute | solution.py:432
  91.0 4.7 %copy-start.12 = (f32[1,2,6,4,320]{4,3,2,1,0:T(4,128)}, f32[1,2,6,4,320]{4,3,2,1,0:T(4,128)S(1)}, u32[]{:S(2)}) copy-start(f32[1,2,6,4,320]{4,3,2,1,0:T(4,128)S(1)} %collective-permute-done.13.refs_7_) | copy-start | bytes 184324
  91.0 28.8 %collective-permute-start.10 = (f32[1,2,6,4,320]{4,3,2,1,0:T(4,128)}, f32[1,2,6,4,320]{4,3,2,1,0:T(4,128)S(1)}, u32[]{:S(2)}, u32[]{:S(2)}) collective-permute-start(f32[1,2,6,4,320]{4,3,2,1,0:T(4,128)} %get-tuple-element.20.refs_4_), channel_id=1, source_target_pairs={{0,2},{1,3},{2,0},{3,1},{4,6},{5,7},{6,4},{7,5},{8,10},{9,11},{10,... | collective-permute-start | bytes 184328 | tf_op jit(solution)/shard_map/ppermute | solution.py:433
  92.1 62.5 %collective-permute-start.15 = (bf16[1,24,192,320]{3,2,1,0:T(8,128)(2,1)}, bf16[1,24,192,320]{3,2,1,0:T(8,128)(2,1)}, u32[]{:S(2)}, u32[]{:S(2)}) collective-permute-start(bf16[1,24,192,320]{3,2,1,0:T(8,128)(2,1)} %get-tuple-element.21.refs_1_.refs_12_), channel_id=1, source_target_pairs={{4,0},{5,1},{6,2},{7,3},{12,8},{13,9},{14,10},{15,11},{20,16},{21,... | collective-permute-start | bytes 8847368 | tf_op jit(solution)/shard_map/ppermute | solution.py:440
  94.1 66.2 %collective-permute-start.7 = (bf16[1,24,192,320]{3,2,1,0:T(8,128)(2,1)}, bf16[1,24,192,320]{3,2,1,0:T(8,128)(2,1)S(1)}, u32[]{:S(2)}, u32[]{:S(2)}) collective-permute-start(bf16[1,24,192,320]{3,2,1,0:T(8,128)(2,1)} %get-tuple-element.17.refs_1_.refs_12_), channel_id=1, source_target_pairs={{4,0},{5,1},{6,2},{7,3},{12,8},{13,9},{14,10},{15,11},{20,16},{21,... | collective-permute-start | bytes 8847368 | tf_op jit(solution)/shard_map/ppermute | solution.py:440
  119.8 7.0 %copy-start.3 = (f32[1,2,6,4,320]{4,3,2,1,0:T(4,128)}, f32[1,2,6,4,320]{4,3,2,1,0:T(4,128)S(1)}, u32[]{:S(2)}) copy-start(f32[1,2,6,4,320]{4,3,2,1,0:T(4,128)S(1)} %collective-permute-done.10.refs_7_) | copy-start | bytes 184324
  119.8 34.8 %collective-permute-start.16 = (bf16[1,24,192,320]{3,2,1,0:T(8,128)(2,1)}, bf16[1,24,192,320]{3,2,1,0:T(8,128)(2,1)}, u32[]{:S(2)}, u32[]{:S(2)}) collective-permute-start(bf16[1,24,192,320]{3,2,1,0:T(8,128)(2,1)} %get-tuple-element.27), channel_id=1, source_target_pairs={{0,4},{1,5},{2,6},{3,7},{8,12},{9,13},{10,14},{11,15},{16,20},{17,... | collective-permute-start | bytes 8847368 | tf_op jit(solution)/shard_map/ppermute | solution.py:446
  151.5 8.8 %collective-permute-start.14 = (bf16[1,24,192,320]{3,2,1,0:T(8,128)(2,1)}, bf16[1,24,192,320]{3,2,1,0:T(8,128)(2,1)}, u32[]{:S(2)}, u32[]{:S(2)}) collective-permute-start(bf16[1,24,192,320]{3,2,1,0:T(8,128)(2,1)} %get-tuple-element.26), channel_id=1, source_target_pairs={{0,4},{1,5},{2,6},{3,7},{8,12},{9,13},{10,14},{11,15},{16,20},{17,... | collective-permute-start | bytes 8847368 | tf_op jit(solution)/shard_map/ppermute | solution.py:446
  160.3 1.7 %copy-start = (bf16[1,24,192,320]{3,2,1,0:T(8,128)(2,1)}, bf16[1,24,192,320]{3,2,1,0:T(8,128)(2,1)S(1)}, u32[]{:S(2)}) copy-start(bf16[1,24,192,320]{3,2,1,0:T(8,128)(2,1)S(1)} %collective-permute-done.7.a_ref) | copy-start | bytes 8847364
  (6 other events, 6.4 us)
